TPU v7x, 128 devices: a whole 4x4x4 slice. The times are simulated.
128 devices in a mesh: rows: 128 (over z, y, x, core).
Axes of the slice: x: 4, y: 4, z: 4, core: 2. Of those that a mesh axis runs over, the one named last changes fastest.
Arguments:
- wave_fn: float32 [640, 4, 4, 640], P('rows')
- left_env: bfloat16 [32, 640, 640], P(None, 'rows')
- op_pair: bfloat16 [32, 16, 16], replicated
- right_env: bfloat16 [32, 640, 640], replicated
Outputs:
- output 1: float32 [7, 640, 4, 4, 640], P(None, 'rows')
- output 2: float32 [6], replicated
- output 3: float32 [6], replicated
All inputs are finite; a program needn't handle non-finite values.
Results may differ from a plain program's by a relative error of at most 0.011815.
Values are sent between devices in bfloat16 or wider.
A program may use at most 1 GiB of HBM per device.

v0:
```python
import jax
import jax.numpy as jnp
from jax import lax
from jax.sharding import PartitionSpec as P

NUM_STEPS = 6


def solution(mesh):
    row_axis = "rows"

    def local_run(wave_rows, left_rows, op_pair, right_env):
        local_rows = wave_rows.shape[0]
        phys_dim = wave_rows.shape[1]
        bond_dim = wave_rows.shape[3]
        num_terms = left_rows.shape[0]
        pair_dim = phys_dim * phys_dim
        vec_count = bond_dim * bond_dim * pair_dim
        right_flat = jnp.transpose(right_env, (0, 2, 1)).reshape(num_terms * bond_dim, bond_dim)

        def matvec(vec_rows):
            whole_vec = lax.all_gather(vec_rows.astype(jnp.bfloat16), row_axis, axis=0, tiled=True)
            flat_in = whole_vec.reshape(bond_dim, pair_dim * bond_dim)
            left_out = jnp.einsum("kap,pn->kan", left_rows, flat_in, preferred_element_type=jnp.float32)
            left_out = left_out.astype(jnp.bfloat16).reshape(num_terms, local_rows, pair_dim, bond_dim)
            mid_out = jnp.einsum("kqr,karc->aqkc", op_pair, left_out, preferred_element_type=jnp.float32)
            mid_out = mid_out.astype(jnp.bfloat16).reshape(local_rows * pair_dim, num_terms * bond_dim)
            sigma_rows = jnp.dot(mid_out, right_flat, preferred_element_type=jnp.float32)
            return sigma_rows.reshape(local_rows, phys_dim, phys_dim, bond_dim)

        def global_mean(local_val):
            return lax.psum(jnp.sum(local_val), row_axis) / vec_count

        first_vec = wave_rows / jnp.sqrt(global_mean(wave_rows * wave_rows))
        prev_vec = jnp.zeros_like(first_vec)
        cur_vec = first_vec
        beta_prev = jnp.zeros((), jnp.float32)
        vec_list = [first_vec]
        alpha_list = []
        beta_list = []
        for step_idx in range(NUM_STEPS):
            sigma_rows = matvec(cur_vec)
            alpha_val = global_mean(sigma_rows * cur_vec)
            resid_vec = sigma_rows - alpha_val * cur_vec - beta_prev * prev_vec
            beta_val = jnp.sqrt(global_mean(resid_vec * resid_vec))
            next_vec = resid_vec / beta_val
            vec_list.append(next_vec)
            alpha_list.append(alpha_val)
            beta_list.append(beta_val)
            prev_vec = cur_vec
            cur_vec = next_vec
            beta_prev = beta_val
        return jnp.stack(vec_list), jnp.stack(alpha_list), jnp.stack(beta_list)

    return jax.shard_map(local_run, mesh=mesh, in_specs=(P(row_axis), P(None, row_axis), P(), P()), out_specs=(P(None, row_axis), P(), P()), check_vma=False)
```

profile of v0, /device:TPU:1, one launch (start us, length us, event | category | flops | bytes accessed | tf_op | source)
XLA Modules:
  0.0 1626.5 jit_solution(12859389179089549338)
XLA Ops:
  7.2 1.7 multiply_reduce_fusion.12
  8.9 68.7 %psum.91 = f32[]{:T(128)} all-reduce(f32[]{:T(128)} %multiply_reduce_fusion.12), channel_id=1, replica_groups=mesh['rows'=128] {'rows'}, use_global_device_ids=true, to_apply=%region_1.0 | all-reduce | flops 1 | bytes 8 | tf_op jit(solution)/shard_map/psum | solution.py:32
  78.3 1.6 fusion.28
  80.0 1.0 copy.89
  81.0 33.9 %copy.63 = bf16[32,640,640]{1,2,0:T(8,128)(2,1)} copy(bf16[32,640,640]{2,1,0:T(8,128)(2,1)} %param.7) | data formatting | bytes 52428800 | tf_op args[3]
  114.9 35.9 %all-gather.7.cloned.1.call-done = bf16[640,4,4,640]{3,2,1,0:T(4,128)(2,1)} async-done(((bf16[5,4,4,640]{3,2,1,0:T(4,128)(2,1)}), bf16[640,4,4,640]{3,2,1,0:T(4,128)(2,1)}) %all-gather.7.cloned.1.call-update) | async-done | bytes 13107216 | tf_op jit(solution)/shard_map/all_gather | solution.py:22
  150.8 19.6 %reshape.82 = bf16[640,10240,1]{1,0,2:T(8,128)(2,1)} reshape(bf16[640,4,4,640]{3,2,1,0:T(4,128)(2,1)} %all-gather.7.cloned.1.call-done) | data formatting | bytes 26214400 | tf_op jit(solution)/shard_map/reshape | solution.py:23
  170.4 7.5 convolution_convert_fusion
  178.6 1.0 convert_bitcast_fusion.5
  180.3 3.2 dot_general.68
  183.4 15.7 multiply_reduce_fusion.11
  199.2 64.7 %psum.92 = f32[]{:T(128)} all-reduce(f32[]{:T(128)} %get-tuple-element.21), channel_id=1, replica_groups=mesh['rows'=128] {'rows'}, use_global_device_ids=true, to_apply=%region_3.0 | all-reduce | flops 1 | bytes 8 | tf_op jit(solution)/shard_map/psum | solution.py:32
  265.3 64.1 %psum.93 = f32[]{:T(128)} all-reduce(f32[]{:T(128)} %multiply_reduce_fusion.10), channel_id=1, replica_groups=mesh['rows'=128] {'rows'}, use_global_device_ids=true, to_apply=%region_5.0 | all-reduce | flops 1 | bytes 8 | tf_op jit(solution)/shard_map/psum | solution.py:32
  330.1 0.8 fusion.29
  330.9 70.8 %all-gather.9.cloned.1.call-done = bf16[640,4,4,640]{3,2,1,0:T(4,128)(2,1)} async-done(((bf16[5,4,4,640]{3,2,1,0:T(4,128)(2,1)}), bf16[640,4,4,640]{3,2,1,0:T(4,128)(2,1)}) %all-gather.9.cloned.1.call-update) | async-done | bytes 13107216 | tf_op jit(solution)/shard_map/all_gather | solution.py:22
  401.7 22.4 %copy.64 = bf16[640,4,4,640]{0,3,2,1:T(8,128)(2,1)} copy(bf16[640,4,4,640]{3,2,1,0:T(4,128)(2,1)} %all-gather.9.cloned.1.call-done) | data formatting | bytes 26214400 | tf_op jit(solution)/shard_map/all_gather | solution.py:22
  424.2 9.1 convolution_convert_fusion.5
  434.2 1.0 convert_bitcast_fusion.4
  435.9 3.2 dot_general.72
  439.1 15.7 multiply_reduce_fusion.9
  454.8 64.5 %psum.94 = f32[]{:T(128)} all-reduce(f32[]{:T(128)} %get-tuple-element.23), channel_id=1, replica_groups=mesh['rows'=128] {'rows'}, use_global_device_ids=true, to_apply=%region_7.0 | all-reduce | flops 1 | bytes 8 | tf_op jit(solution)/shard_map/psum | solution.py:32
  519.9 0.7 multiply_reduce_fusion.8
  520.7 74.0 %psum.95 = f32[]{:T(128)} all-reduce(f32[]{:T(128)} %get-tuple-element.17), channel_id=1, replica_groups=mesh['rows'=128] {'rows'}, use_global_device_ids=true, to_apply=%region_9.0 | all-reduce | flops 1 | bytes 8 | tf_op jit(solution)/shard_map/psum | solution.py:32
  596.1 70.8 %all-gather.11.cloned.1.call-done = bf16[640,4,4,640]{3,2,1,0:T(4,128)(2,1)} async-done(((bf16[5,4,4,640]{3,2,1,0:T(4,128)(2,1)}), bf16[640,4,4,640]{3,2,1,0:T(4,128)(2,1)}) %all-gather.11.cloned.1.call-update) | async-done | bytes 13107216 | tf_op jit(solution)/shard_map/all_gather | solution.py:22
  666.9 22.4 %copy.69 = bf16[640,4,4,640]{0,3,2,1:T(8,128)(2,1)} copy(bf16[640,4,4,640]{3,2,1,0:T(4,128)(2,1)} %all-gather.11.cloned.1.call-done) | data formatting | bytes 26214400 | tf_op jit(solution)/shard_map/all_gather | solution.py:22
  689.3 9.1 convolution_convert_fusion.4
  699.4 1.0 convert_bitcast_fusion.3
  701.1 3.2 dot_general.76
  704.2 15.7 multiply_reduce_fusion.7
  720.0 64.5 %psum.96 = f32[]{:T(128)} all-reduce(f32[]{:T(128)} %get-tuple-element.25), channel_id=1, replica_groups=mesh['rows'=128] {'rows'}, use_global_device_ids=true, to_apply=%region_11.0 | all-reduce | flops 1 | bytes 8 | tf_op jit(solution)/shard_map/psum | solution.py:32
  785.1 0.7 multiply_reduce_fusion.6
  785.9 64.1 %psum.97 = f32[]{:T(128)} all-reduce(f32[]{:T(128)} %get-tuple-element.15), channel_id=1, replica_groups=mesh['rows'=128] {'rows'}, use_global_device_ids=true, to_apply=%region_13.0 | all-reduce | flops 1 | bytes 8 | tf_op jit(solution)/shard_map/psum | solution.py:32
  851.8 70.4 %all-gather.13.cloned.1.call-done = bf16[640,4,4,640]{3,2,1,0:T(4,128)(2,1)} async-done(((bf16[5,4,4,640]{3,2,1,0:T(4,128)(2,1)}), bf16[640,4,4,640]{3,2,1,0:T(4,128)(2,1)}) %all-gather.13.cloned.1.call-update) | async-done | bytes 13107216 | tf_op jit(solution)/shard_map/all_gather | solution.py:22
  922.2 22.4 %copy.74 = bf16[640,4,4,640]{0,3,2,1:T(8,128)(2,1)} copy(bf16[640,4,4,640]{3,2,1,0:T(4,128)(2,1)} %all-gather.13.cloned.1.call-done) | data formatting | bytes 26214400 | tf_op jit(solution)/shard_map/all_gather | solution.py:22
  944.6 9.1 convolution_convert_fusion.3
  954.7 1.0 convert_bitcast_fusion.2
  956.4 3.2 dot_general.80
  959.5 15.7 multiply_reduce_fusion.5
  975.3 64.5 %psum.98 = f32[]{:T(128)} all-reduce(f32[]{:T(128)} %get-tuple-element.27), channel_id=1, replica_groups=mesh['rows'=128] {'rows'}, use_global_device_ids=true, to_apply=%region_15.0 | all-reduce | flops 1 | bytes 8 | tf_op jit(solution)/shard_map/psum | solution.py:32
  1040.4 0.7 multiply_reduce_fusion.4
  1041.2 64.3 %psum.99 = f32[]{:T(128)} all-reduce(f32[]{:T(128)} %get-tuple-element.13), channel_id=1, replica_groups=mesh['rows'=128] {'rows'}, use_global_device_ids=true, to_apply=%region_17.0 | all-reduce | flops 1 | bytes 8 | tf_op jit(solution)/shard_map/psum | solution.py:32
  1106.9 70.8 %all-gather.15.cloned.1.call-done = bf16[640,4,4,640]{3,2,1,0:T(4,128)(2,1)} async-done(((bf16[5,4,4,640]{3,2,1,0:T(4,128)(2,1)}), bf16[640,4,4,640]{3,2,1,0:T(4,128)(2,1)}) %all-gather.15.cloned.1.call-update) | async-done | bytes 13107216 | tf_op jit(solution)/shard_map/all_gather | solution.py:22
  1177.7 22.4 %copy.79 = bf16[640,4,4,640]{0,3,2,1:T(8,128)(2,1)} copy(bf16[640,4,4,640]{3,2,1,0:T(4,128)(2,1)} %all-gather.15.cloned.1.call-done) | data formatting | bytes 26214400 | tf_op jit(solution)/shard_map/all_gather | solution.py:22
  1200.2 9.1 convolution_convert_fusion.2
  1210.2 1.0 convert_bitcast_fusion.1
  1211.9 3.2 dot_general.84
  1215.1 15.8 multiply_reduce_fusion.3
  1230.9 64.5 %psum.100 = f32[]{:T(128)} all-reduce(f32[]{:T(128)} %get-tuple-element.29), channel_id=1, replica_groups=mesh['rows'=128] {'rows'}, use_global_device_ids=true, to_apply=%region_19.0 | all-reduce | flops 1 | bytes 8 | tf_op jit(solution)/shard_map/psum | solution.py:32
  1296.0 0.7 multiply_reduce_fusion.2
  1296.8 64.3 %psum.101 = f32[]{:T(128)} all-reduce(f32[]{:T(128)} %get-tuple-element.11), channel_id=1, replica_groups=mesh['rows'=128] {'rows'}, use_global_device_ids=true, to_apply=%region_21.0 | all-reduce | flops 1 | bytes 8 | tf_op jit(solution)/shard_map/psum | solution.py:32
  1362.5 0.7 bitcast_dynamic-update-slice_fusion.6
  1363.9 0.7 bitcast_dynamic-update-slice_fusion.4
  1364.6 0.7 bitcast_dynamic-update-slice_fusion.3
  1365.3 0.7 bitcast_dynamic-update-slice_fusion.2
  1366.7 66.5 %all-gather.17.cloned.1.call-done = bf16[640,4,4,640]{3,2,1,0:T(4,128)(2,1)} async-done(((bf16[5,4,4,640]{3,2,1,0:T(4,128)(2,1)}), bf16[640,4,4,640]{3,2,1,0:T(4,128)(2,1)}) %all-gather.17.cloned.1.call-update) | async-done | bytes 13107216 | tf_op jit(solution)/shard_map/all_gather | solution.py:22
  1433.3 22.4 %copy.84 = bf16[640,4,4,640]{0,3,2,1:T(8,128)(2,1)} copy(bf16[640,4,4,640]{3,2,1,0:T(4,128)(2,1)} %all-gather.17.cloned.1.call-done) | data formatting | bytes 26214400 | tf_op jit(solution)/shard_map/all_gather | solution.py:22
  1455.7 9.1 convolution_convert_fusion.1
  1465.8 1.0 convert_bitcast_fusion
  1467.5 3.2 dot_general.88
  1470.6 15.7 multiply_reduce_fusion.1
  1486.4 64.7 %psum.102 = f32[]{:T(128)} all-reduce(f32[]{:T(128)} %get-tuple-element.31), channel_id=1, replica_groups=mesh['rows'=128] {'rows'}, use_global_device_ids=true, to_apply=%region_23.0 | all-reduce | flops 1 | bytes 8 | tf_op jit(solution)/shard_map/psum | solution.py:32
  1551.8 0.7 multiply_reduce_fusion
  1552.5 64.1 %psum.103 = f32[]{:T(128)} all-reduce(f32[]{:T(128)} %get-tuple-element.9), channel_id=1, replica_groups=mesh['rows'=128] {'rows'}, use_global_device_ids=true, to_apply=%region_25.0 | all-reduce | flops 1 | bytes 8 | tf_op jit(solution)/shard_map/psum | solution.py:32
  1617.3 0.7 bitcast_dynamic-update-slice_fusion
  (83 shorter events, 16.1 us)
Async XLA Ops:
  7.2 163.3 %copy-start = (bf16[32,5,640]{2,0,1:T(8,128)(2,1)S(1)}, bf16[32,5,640]{2,0,1:T(8,128)(2,1)}, u32[]{:S(2)}) copy-start(bf16[32,5,640]{2,0,1:T(8,128)(2,1)} %param.5) | copy-start | bytes 614404
  7.2 143.6 %all-gather.7.cloned.1.call-start = ((), (), s32[]{:S(2)}) async-start(), calls=%async_computation | async-start | bytes 13209600 | tf_op jit(solution)/shard_map/all_gather | solution.py:22
  79.9 321.8 %all-gather.9.cloned.1.call-start = ((), (), s32[]{:S(2)}) async-start(), calls=%async_computation.1 | async-start | bytes 13209600 | tf_op jit(solution)/shard_map/all_gather | solution.py:22
  81.0 97.6 %copy-start.4 = (bf16[32,16,16,1]{2,1,3,0:T(8,128)(2,1)}, bf16[32,16,16,1]{2,1,3,0:T(8,128)(2,1)S(1)}, u32[]{:S(2)}) copy-start(bf16[32,16,16,1]{2,1,3,0:T(8,128)(2,1)S(1)} %copy.89) | copy-start | bytes 49156
  183.4 81.1 %copy-start.1 = (f32[5,4,4,640]{3,2,1,0:T(4,128)S(1)}, f32[5,4,4,640]{3,2,1,0:T(4,128)}, u32[]{:S(2)}) copy-start(f32[5,4,4,640]{3,2,1,0:T(4,128)} %param.4) | copy-start | bytes 614404
  330.9 336.0 %all-gather.11.cloned.1.call-start = ((), (), s32[]{:S(2)}) async-start(), calls=%async_computation.2 | async-start | bytes 13209600 | tf_op jit(solution)/shard_map/all_gather | solution.py:22
  433.3 0.9 copy-start.5
  439.1 80.9 %copy-start.2 = (f32[5,4,4,640]{3,2,1,0:T(4,128)S(1)}, f32[5,4,4,640]{3,2,1,0:T(4,128)}, u32[]{:S(2)}) copy-start(f32[5,4,4,640]{3,2,1,0:T(4,128)} %param.4) | copy-start | bytes 614404
  439.1 80.9 %copy-start.20 = (f32[5,4,4,640]{3,2,1,0:T(4,128)S(1)}, f32[5,4,4,640]{3,2,1,0:T(4,128)}, u32[]{:S(2)}) copy-start(f32[5,4,4,640]{3,2,1,0:T(4,128)} %get-tuple-element.20) | copy-start | bytes 614404
  520.7 168.7 %copy-start.10 = (f32[5,4,4,640]{3,2,1,0:T(4,128)}, f32[5,4,4,640]{3,2,1,0:T(4,128)S(1)}, u32[]{:S(2)}) copy-start(f32[5,4,4,640]{3,2,1,0:T(4,128)S(1)} %get-tuple-element.18) | copy-start | bytes 614404
  596.1 326.1 %all-gather.13.cloned.1.call-start = ((), (), s32[]{:S(2)}) async-start(), calls=%async_computation.3 | async-start | bytes 13209600 | tf_op jit(solution)/shard_map/all_gather | solution.py:22
  698.5 0.9 copy-start.6
  704.2 80.9 %copy-start.11 = (f32[5,4,4,640]{3,2,1,0:T(4,128)S(1)}, f32[5,4,4,640]{3,2,1,0:T(4,128)}, u32[]{:S(2)}) copy-start(f32[5,4,4,640]{3,2,1,0:T(4,128)} %copy-done.10) | copy-start | bytes 614404
  704.2 80.9 %copy-start.21 = (f32[5,4,4,640]{3,2,1,0:T(4,128)S(1)}, f32[5,4,4,640]{3,2,1,0:T(4,128)}, u32[]{:S(2)}) copy-start(f32[5,4,4,640]{3,2,1,0:T(4,128)} %get-tuple-element.20) | copy-start | bytes 614404
  785.9 158.8 %copy-start.14 = (f32[5,4,4,640]{3,2,1,0:T(4,128)}, f32[5,4,4,640]{3,2,1,0:T(4,128)S(1)}, u32[]{:S(2)}) copy-start(f32[5,4,4,640]{3,2,1,0:T(4,128)S(1)} %get-tuple-element.16) | copy-start | bytes 614404
  851.4 326.3 %all-gather.15.cloned.1.call-start = ((), (), s32[]{:S(2)}) async-start(), calls=%async_computation.4 | async-start | bytes 13209600 | tf_op jit(solution)/shard_map/all_gather | solution.py:22
  953.8 0.9 copy-start.7
  959.5 80.9 %copy-start.12 = (f32[5,4,4,640]{3,2,1,0:T(4,128)S(1)}, f32[5,4,4,640]{3,2,1,0:T(4,128)}, u32[]{:S(2)}) copy-start(f32[5,4,4,640]{3,2,1,0:T(4,128)} %copy-done.10) | copy-start | bytes 614404
  959.5 80.9 %copy-start.15 = (f32[5,4,4,640]{3,2,1,0:T(4,128)S(1)}, f32[5,4,4,640]{3,2,1,0:T(4,128)}, u32[]{:S(2)}) copy-start(f32[5,4,4,640]{3,2,1,0:T(4,128)} %copy-done.14) | copy-start | bytes 614404
  1041.2 159.0 %copy-start.17 = (f32[5,4,4,640]{3,2,1,0:T(4,128)}, f32[5,4,4,640]{3,2,1,0:T(4,128)S(1)}, u32[]{:S(2)}) copy-start(f32[5,4,4,640]{3,2,1,0:T(4,128)S(1)} %get-tuple-element.14) | copy-start | bytes 614404
  1106.9 326.4 %all-gather.17.cloned.1.call-start = ((), (), s32[]{:S(2)}) async-start(), calls=%async_computation.5 | async-start | bytes 13209600 | tf_op jit(solution)/shard_map/all_gather | solution.py:22
  1209.3 0.9 copy-start.8
  1215.1 80.9 %copy-start.16 = (f32[5,4,4,640]{3,2,1,0:T(4,128)S(1)}, f32[5,4,4,640]{3,2,1,0:T(4,128)}, u32[]{:S(2)}) copy-start(f32[5,4,4,640]{3,2,1,0:T(4,128)} %copy-done.14) | copy-start | bytes 614404
  1215.1 80.9 %copy-start.18 = (f32[5,4,4,640]{3,2,1,0:T(4,128)S(1)}, f32[5,4,4,640]{3,2,1,0:T(4,128)}, u32[]{:S(2)}) copy-start(f32[5,4,4,640]{3,2,1,0:T(4,128)} %copy-done.17) | copy-start | bytes 614404
  1215.1 147.4 %copy-start.3 = (f32[5,4,4,640]{3,2,1,0:T(4,128)S(1)}, f32[5,4,4,640]{3,2,1,0:T(4,128)}, u32[]{:S(2)}) copy-start(f32[5,4,4,640]{3,2,1,0:T(4,128)} %param.4) | copy-start | bytes 614404
  1215.1 148.1 %copy-start.22 = (f32[5,4,4,640]{3,2,1,0:T(4,128)S(1)}, f32[5,4,4,640]{3,2,1,0:T(4,128)}, u32[]{:S(2)}) copy-start(f32[5,4,4,640]{3,2,1,0:T(4,128)} %get-tuple-element.20) | copy-start | bytes 614404
  1215.1 148.8 %copy-start.13 = (f32[5,4,4,640]{3,2,1,0:T(4,128)S(1)}, f32[5,4,4,640]{3,2,1,0:T(4,128)}, u32[]{:S(2)}) copy-start(f32[5,4,4,640]{3,2,1,0:T(4,128)} %copy-done.10) | copy-start | bytes 614404
  1296.8 159.0 %copy-start.23 = (f32[5,4,4,640]{3,2,1,0:T(4,128)}, f32[5,4,4,640]{3,2,1,0:T(4,128)S(1)}, u32[]{:S(2)}) copy-start(f32[5,4,4,640]{3,2,1,0:T(4,128)S(1)} %get-tuple-element.12) | copy-start | bytes 614404
  1464.9 0.9 copy-start.9
  1470.6 81.1 %copy-start.19 = (f32[5,4,4,640]{3,2,1,0:T(4,128)S(1)}, f32[5,4,4,640]{3,2,1,0:T(4,128)}, u32[]{:S(2)}) copy-start(f32[5,4,4,640]{3,2,1,0:T(4,128)} %copy-done.17) | copy-start | bytes 614404
  1470.6 81.1 %copy-start.24 = (f32[5,4,4,640]{3,2,1,0:T(4,128)S(1)}, f32[5,4,4,640]{3,2,1,0:T(4,128)}, u32[]{:S(2)}) copy-start(f32[5,4,4,640]{3,2,1,0:T(4,128)} %copy-done.23) | copy-start | bytes 614404
Sparse Core Ops, SparseCore 0:
  80.1 70.7 all-gather.6
  331.0 70.6 all-gather.8
  596.2 70.6 all-gather.10
  851.5 70.6 all-gather.12
  1107.0 70.6 all-gather.14
  1362.6 70.6 all-gather.16
where the time goes:
time: 1640 us; the launch traced here: 1630 us
  blocking collectives  851 us (52%)
  waiting for transfers between devices  385 us (23%)
  local copies, waits for them, and re-layouts  197 us (12%)
  matrix products  154 us (9%)
  between operations  23.7 us (1%)
    psum x13, blocking collectives, global_mean(): return lax.psum(jnp.sum(local_val), row_axis) / vec_count  851 us
    all_gather x6, waiting for transfers between devices, matvec(): lax.all_gather(vec_rows.astype(jnp.bfloat16), row_axis, axis=0, tiled=True)  385 us
    all_gather x5, local copies, waits for them, and re-layouts, matvec(): lax.all_gather(vec_rows.astype(jnp.bfloat16), row_axis, axis=0, tiled=True)  112 us
    dot_general x6, matrix products, matvec(): jnp.dot(mid_out, right_flat, preferred_element_type=jnp.float32)  94.5 us
    dot_general x6, matrix products, matvec(): jnp.einsum('kap,pn->kan', left_rows, flat_in, preferred_element_type=jnp....  53.1 us
    unnamed x59, local copies, waits for them, and re-layouts  40.8 us
  transfers between devices with their start and end apart: 6, of which 6 were waited for; matrix products, arithmetic and copies ran while one was open for 2% of the time, Pallas kernels for 0%

commit v1 on v0

v1 whole, which is shorter than its diff:
```python
import functools

import jax
import jax.numpy as jnp
from jax import lax
from jax.experimental import pallas as pl
from jax.experimental.pallas import tpu as pltpu
from jax.sharding import PartitionSpec as P

NUM_STEPS = 6
MESH = pl.DeviceIdType.MESH
F32 = jnp.float32
BF16 = jnp.bfloat16

GA, GC = 16, 8
ROWS, COLS = 40, 80
BOND, PAIR, TERMS = 640, 16, 32
LANES = 128
VEC = BOND * BOND * PAIR


def remote(src, dst, send, recv, dev):
    return pltpu.make_async_remote_copy(src_ref=src, dst_ref=dst, send_sem=send, recv_sem=recv, device_id=(dev,), device_id_type=MESH)


def lane_roll(val, shift):
    shift = shift % LANES
    return val if shift == 0 else pltpu.roll(val, shift, axis=val.ndim - 1)


def lane_iota(val):
    return lax.broadcasted_iota(jnp.int32, val.shape, val.ndim - 1)


def take_piece(tiles, idx):
    tile, off = divmod(COLS * idx, LANES)
    out = lane_roll(tiles(tile), -off)
    lane = lane_iota(out)
    if off + COLS > LANES:
        out = jnp.where(lane < LANES - off, out, lane_roll(tiles(tile + 1), -off))
    return jnp.where(lane < COLS, out, jnp.zeros_like(out))


def dense_tile(pieces, tile):
    out = None
    for idx in range(8):
        shift = COLS * idx - LANES * tile
        if shift <= -COLS or shift >= LANES:
            continue
        moved = lane_roll(pieces(idx), shift)
        out = moved if out is None else jnp.where(lane_iota(moved) >= shift, moved, out)
    return out


def kernel(psi, lw, wbig, right, vecs, alphas, betas, lall, lh, rtmp, rt, ug, xs, ys, part, rd, ssum, ra, rb, fl, fr, fin,
           sig, vt, piece_buf, out_recv, outv, ar1, ar2, psi_s, psi_r, l_s, l_r, lf_s, lf_r, out_s, out_r, g_s, g_r, d_s, d_r,
           ring_s, ring_r, a1_s, a1_r, a2_s, a2_r, loc):
    me = lax.axis_index("rows")
    core = lax.rem(me, 2)
    x = lax.rem(me // 2, 4)
    y = lax.rem(me // 8, 4)
    z = me // 32
    i = me // 8
    j = lax.rem(me, 8)

    def in_row(dj):
        jj = lax.rem(j + dj, 8)
        return jj, i * 8 + jj

    def in_col(di):
        ii = lax.rem(i + di, PAIR)
        return ii, ii * 8 + j

    barrier = pltpu.get_barrier_semaphore()
    for dj in range(1, 8):
        pl.semaphore_signal(barrier, inc=1, device_id=(in_row(dj)[1],), device_id_type=MESH)
    for di in range(1, PAIR):
        pl.semaphore_signal(barrier, inc=1, device_id=(in_col(di)[1],), device_id_type=MESH)
    pl.semaphore_wait(barrier, 22)

    partner = me + 1 - 2 * core
    xdev = lambda xx: i * 8 + lax.rem(xx + 4, 4) * 2 + core

    cp_r = pltpu.make_async_copy(right.at[:, pl.ds(pl.multiple_of(j * COLS, COLS), COLS), :], rtmp.at[:, pl.ds(0, COLS), :], loc.at[0])
    cp_r.start()
    cp_l = pltpu.make_async_copy(lw, lall.at[j], loc.at[1])
    cp_l.start()

    for jj in range(8):
        piece_buf[jj] = take_piece(lambda t: psi[:, LANES * t:LANES * t + LANES], jj)
    my_rows = pl.ds(pl.multiple_of(j * COLS, COLS), COLS)
    vt[0, my_rows, :] = piece_buf[j]
    psi_copies = []
    for dj in range(1, 8):
        jj, dev = in_row(dj)
        cp = remote(piece_buf.at[jj], vt.at[0, my_rows], psi_s.at[jj], psi_r.at[j], dev)
        cp.start()
        psi_copies.append(cp)
    l_copies = []
    for dx in range(1, 4):
        xx = lax.rem(x + dx, 4)
        cp = remote(lw, lall.at[j], l_s.at[xx], l_r.at[x], i * 8 + xx * 2 + core)
        cp.start()
        l_copies.append(cp)
    cp = remote(lw, lall.at[j], lf_s.at[x], lf_r.at[x], partner)
    cp.start()
    l_copies.append(cp)

    row_lane = lax.broadcasted_iota(jnp.int32, (1, LANES), 1)

    def total(val):
        return jnp.sum(jnp.sum(val, axis=0, keepdims=True), axis=1, keepdims=True)

    def pack_row(n, s, e, c):
        zero = jnp.zeros((1, LANES), F32)
        return jnp.where(row_lane == 0, n, jnp.where(row_lane == 1, s, jnp.where(row_lane == 2, e, jnp.where(row_lane == 3, c, zero))))

    def merge(mat):
        lane = lax.broadcasted_iota(jnp.int32, mat.shape, 2)
        col = lambda idx: jnp.sum(jnp.where(lane == idx, mat, 0.0), axis=2, keepdims=True)
        n, s, e, c = col(0), col(1), col(2), col(3)
        mean = jnp.where(n > 0, s / jnp.where(n > 0, n, 1.0), 0.0)
        n_all, s_all, c_all = (jnp.sum(val, axis=0, keepdims=True) for val in (n, s, c))
        mean_all = jnp.where(n_all > 0, s_all / jnp.where(n_all > 0, n_all, 1.0), 0.0)
        diff = mean - mean_all
        e_all = jnp.sum(e + diff * n * diff, axis=0, keepdims=True)
        return tuple(val.reshape(1, 1) for val in (n_all, s_all, e_all, c_all))

    def all_reduce(n, s, e, c):
        ar1[j] = pack_row(n, s, e, c)
        copies = []
        for dj in range(1, 8):
            jj, dev = in_row(dj)
            cp = remote(ar1.at[j], ar1.at[j], a1_s.at[jj], a1_r.at[j], dev)
            cp.start()
            copies.append(cp)
        for dj in range(1, 8):
            jj, dev = in_row(dj)
            remote(ar1.at[jj], ar1.at[jj], a1_s.at[jj], a1_r.at[jj], dev).wait_recv()
        n, s, e, c = merge(ar1[...])
        ar2[i] = pack_row(n, s, e, c)
        for di in range(1, PAIR):
            ii, dev = in_col(di)
            cp = remote(ar2.at[i], ar2.at[i], a2_s.at[ii], a2_r.at[i], dev)
            cp.start()
            copies.append(cp)
        for di in range(1, PAIR):
            ii, dev = in_col(di)
            remote(ar2.at[ii], ar2.at[ii], a2_s.at[ii], a2_r.at[ii], dev).wait_recv()
        for cp in copies:
            cp.wait_send()
        return merge(ar2[...])

    psi_val = psi[...]
    n_psi = total(psi_val * psi_val)
    zero11 = jnp.zeros((1, 1), F32)
    n_psi = all_reduce(n_psi, zero11, zero11, zero11)[0]
    inv_norm = 1.0 / jnp.sqrt(n_psi / VEC)

    for dj in range(1, 8):
        jj, dev = in_row(dj)
        rows = pl.ds(pl.multiple_of(jj * COLS, COLS), COLS)
        remote(piece_buf.at[jj], vt.at[0, rows], psi_s.at[jj], psi_r.at[jj], dev).wait_recv()
    for cp in psi_copies:
        cp.wait_send()
    vt[0] = vt[0] * inv_norm
    vt[2] = jnp.zeros((BOND, LANES), F32)
    fin[...] = jnp.zeros((LANES, BOND), F32)

    cp_r.wait()
    def turn_right(k, carry):
        rtmp[k, pl.ds(COLS, 48), :] = jnp.zeros((48, BOND), BF16)
        for b in range(5):
            rt[pl.ds(LANES * b, LANES), pl.ds(pl.multiple_of(k * LANES, LANES), LANES)] = rtmp[k, :, pl.ds(LANES * b, LANES)].T
        return carry

    lax.fori_loop(0, TERMS, turn_right, 0)

    cp_l.wait()
    fwd = []
    for dx in range(1, 4):
        xx = lax.rem(x + dx, 4)
        src = xx * 2 + core
        remote(lw, lall.at[src], l_s.at[xx], l_r.at[xx], i * 8 + src).wait_recv()
        cp = remote(lall.at[src], lall.at[src], lf_s.at[xx], lf_r.at[xx], partner)
        cp.start()
        fwd.append(cp)
    for xx in range(4):
        src = xx * 2 + 1 - core
        remote(lw, lall.at[src], lf_s.at[xx], lf_r.at[xx], partner).wait_recv()
    for cp in l_copies + fwd:
        cp.wait_send()
    for t in range(8):
        block = lall[t]
        lane = lane_iota(block)
        for h in range(2):
            keep = (lane < 512) | (((lane // 8) % 2) == h)
            lh[h, pl.ds(160 * t, 160), :] = jnp.where(keep, block, jnp.zeros_like(block))

    def ring_ids(half, phase):
        base = half * 8 + phase * 4
        return base, base + 1, base + 2, base + 3

    def gather_phase(up, down, own, blocks, halves, ids):
        to_up, to_dn, fw_up, fw_dn = ids
        from_dn, from_up, far = blocks
        sends = [remote(own(None), own(None), g_s.at[to_up], g_r.at[to_up], up), remote(own(None), own(None), g_s.at[to_dn], g_r.at[to_dn], down)]
        for cp in sends:
            cp.start()

        def forward():
            remote(from_dn(None), from_dn(None), g_s.at[to_up], g_r.at[to_up], up).wait_recv()
            one = remote(from_dn(halves[0]), from_dn(halves[0]), g_s.at[fw_up], g_r.at[fw_up], up)
            one.start()
            remote(from_up(None), from_up(None), g_s.at[to_dn], g_r.at[to_dn], down).wait_recv()
            two = remote(from_up(halves[1]), from_up(halves[1]), g_s.at[fw_dn], g_r.at[fw_dn], down)
            two.start()
            sends.extend([one, two])

        def finish():
            remote(far(halves[0]), far(halves[0]), g_s.at[fw_up], g_r.at[fw_up], up).wait_recv()
            remote(far(halves[1]), far(halves[1]), g_s.at[fw_dn], g_r.at[fw_dn], down).wait_recv()

        return sends, forward, finish

    def wrap4(val):
        return lax.rem(val + 4, 4)

    y_up, y_dn = (z * 4 + wrap4(y + 1)) * 8 + j, (z * 4 + wrap4(y - 1)) * 8 + j
    z_up, z_dn = (wrap4(z + 1) * 4 + y) * 8 + j, (wrap4(z - 1) * 4 + y) * 8 + j
    PARTS = (((0, 12), (0, 6), (6, 6)), ((12, 13), (12, 6), (18, 7)))

    def gather():
        def one(zz, yy, whole):
            def ref(part):
                lo, cnt = part or whole
                return ug.at[zz, yy, pl.ds(lo, cnt)]
            return ref

        def z_bundle(zz, whole):
            def ref(part):
                lo, cnt = part or whole
                return ug.at[zz, :, pl.ds(lo, cnt)]
            return ref

        def y_bundle(yy, whole):
            def ref(part):
                lo, cnt = part or whole
                return ug.at[:, yy, pl.ds(lo, cnt)]
            return ref

        wa, wb = PARTS[0][0], PARTS[1][0]
        ha, hb = PARTS[0][1:], PARTS[1][1:]
        a1 = gather_phase(y_up, y_dn, one(z, y, wa), (one(z, wrap4(y - 1), wa), one(z, wrap4(y + 1), wa), one(z, wrap4(y + 2), wa)), ha, ring_ids(0, 0))
        b1 = gather_phase(z_up, z_dn, one(z, y, wb), (one(wrap4(z - 1), y, wb), one(wrap4(z + 1), y, wb), one(wrap4(z + 2), y, wb)), hb, ring_ids(1, 0))
        a1[1]()
        b1[1]()
        a1[2]()
        a2 = gather_phase(z_up, z_dn, z_bundle(z, wa), (z_bundle(wrap4(z - 1), wa), z_bundle(wrap4(z + 1), wa), z_bundle(wrap4(z + 2), wa)), ha, ring_ids(0, 1))
        b1[2]()
        b2 = gather_phase(y_up, y_dn, y_bundle(y, wb), (y_bundle(wrap4(y - 1), wb), y_bundle(wrap4(y + 1), wb), y_bundle(wrap4(y + 2), wb)), hb, ring_ids(1, 1))
        a2[1]()
        b2[1]()
        a2[2]()
        b2[2]()
        for ph in (a1, b1, a2, b2):
            for cp in ph[0]:
                cp.wait_send()

    def out_start(buf):
        copies = []
        for dj in range(1, 8):
            jj, dev = in_row(dj)
            rows = pl.ds(pl.multiple_of(jj * COLS, COLS), COLS)
            cp = remote(vt.at[buf, rows], out_recv.at[j], out_s.at[jj], out_r.at[j], dev)
            cp.start()
            copies.append(cp)
        out_recv[j] = vt[buf, my_rows, :]
        return copies

    def out_finish(copies, buf, step):
        for dj in range(1, 8):
            jj, dev = in_row(dj)
            rows = pl.ds(pl.multiple_of(jj * COLS, COLS), COLS)
            remote(vt.at[buf, rows], out_recv.at[jj], out_s.at[jj], out_r.at[jj], dev).wait_recv()
        for tile in range(5):
            outv[:, pl.ds(LANES * tile, LANES)] = dense_tile(lambda idx: out_recv[idx], tile)
        cp = pltpu.make_async_copy(outv, vecs.at[step], loc.at[2])
        cp.start()
        for other in copies:
            other.wait_send()
        return cp

    def step_body(step, beta):
        cur = lax.rem(step, 3)
        prev = lax.rem(step + 2, 3)
        nxt = lax.rem(step + 1, 3)

        strided = [vt[cur, pl.ds(r, ROWS, stride=PAIR), :] for r in range(PAIR)]
        for lt in range(5):
            half = [dense_tile(lambda idx, h=h: strided[8 * h + idx], lt) for h in range(2)]
            for h in range(2):
                for tt in range(2):
                    ug[z, y, lt * 5 + 2 * h + tt] = half[h][PAIR * tt:PAIR * tt + PAIR].astype(BF16)
            ug[z, y, lt * 5 + 4] = jnp.concatenate([half[0][32:ROWS], half[1][32:ROWS]], axis=0).astype(BF16)
        gather()
        out_copies = out_start(cur)
        v_cur = vt[cur]
        n_loc = total(v_cur * v_cur)
        c_loc = total(v_cur * vt[prev])

        def left_half(h, carry):
            def tiles(tr, lt):
                return ug[:, :, lt * 5 + tr].reshape(256, LANES)

            for rp in range(4):
                cols = []
                for rr in range(2):
                    idx = 2 * rp + rr
                    tail = take_piece(lambda t: tiles(4, t), idx)
                    main = [take_piece(lambda t, tt=tt: ug[:, :, t * 5 + 2 * h + tt].reshape(256, LANES), idx) for tt in range(2)]
                    cols.append(jnp.concatenate([main[0], main[1], tail], axis=0))
                rhs = jnp.concatenate(cols, axis=1)
                for mc in range(2):
                    res = jnp.dot(lh[h, pl.ds(BOND * mc, BOND), :], rhs, preferred_element_type=F32).astype(BF16)
                    for rr in range(2):
                        xs[h * 8 + 2 * rp + rr, pl.ds(BOND * mc, BOND), :] = res[:, LANES * rr:LANES * rr + LANES]
            return carry

        lax.fori_loop(0, 2, left_half, 0)

        def pair_rows(ap, carry):
            for h in range(2):
                rhs = jnp.concatenate([xs[:, pl.ds(pl.multiple_of(ap * 64 + 32 * aa + PAIR * h, PAIR), PAIR), :].reshape(256, LANES) for aa in range(2)], axis=1)
                res = jnp.dot(wbig[h], rhs, preferred_element_type=F32).astype(BF16)
                for aa in range(2):
                    for k in range(PAIR):
                        ys[pl.ds(pl.multiple_of(ap * 32 + PAIR * aa, PAIR), PAIR), pl.ds((PAIR * h + k) * LANES, LANES)] = res[PAIR * k:PAIR * k + PAIR, LANES * aa:LANES * aa + LANES]
            return carry

        lax.fori_loop(0, ROWS // 2, pair_rows, 0)

        for mc in range(2):
            res = lax.dot_general(rt[pl.ds(320 * mc, 320), :], ys[...], (((1,), (1,)), ((), ())), preferred_element_type=F32)
            for xx in range(2):
                for cc in range(2):
                    lo = (2 * xx + cc) * COLS
                    part[2 * mc + xx, cc] = res[lo:lo + COLS]

        cp_d = remote(part.at[:, 1 - core], rd, d_s, d_r, partner)
        cp_d.start()
        cp_o = out_finish(out_copies, cur, step)
        cp_d.wait()
        for xx in range(4):
            ssum[xx] = part[xx, core] + rd[xx]
        xo, xu, xd = wrap4(x + 2), wrap4(x + 1), wrap4(x - 1)
        up, dn = xdev(x + 1), xdev(x - 1)
        lo, hi = pl.ds(0, ROWS), pl.ds(ROWS, ROWS)
        c0 = remote(ssum.at[xo, lo], ra, ring_s.at[0], ring_r.at[0], up)
        c1 = remote(ssum.at[xo, hi], rb, ring_s.at[1], ring_r.at[1], dn)
        c2 = remote(ssum.at[xu, hi], fl.at[hi], ring_s.at[2], ring_r.at[2], up)
        c3 = remote(ssum.at[xd, lo], fr.at[lo], ring_s.at[3], ring_r.at[3], dn)
        for cp in (c0, c1, c2, c3):
            cp.start()
        c0.wait_recv()
        ssum[xu, lo] = ssum[xu, lo] + ra[...]
        c4 = remote(ssum.at[xu, lo], fl.at[lo], ring_s.at[4], ring_r.at[4], up)
        c4.start()
        c1.wait_recv()
        ssum[xd, hi] = ssum[xd, hi] + rb[...]
        c5 = remote(ssum.at[xd, hi], fr.at[hi], ring_s.at[5], ring_r.at[5], dn)
        c5.start()
        cp_o.wait()
        c2.wait_recv()
        c3.wait_recv()
        c4.wait_recv()
        c5.wait_recv()
        fin[pl.ds(0, COLS), :] = ssum[x] + fl[...] + fr[...]
        for cp in (c0, c1, c2, c3, c4, c5):
            cp.wait_send()
        for b in range(5):
            sig[pl.ds(LANES * b, LANES), :] = fin[:, pl.ds(LANES * b, LANES)].T

        t_val = sig[...] - beta * vt[prev]
        s_loc = total(t_val * vt[cur])
        own = jnp.where(n_loc > 0, s_loc / jnp.where(n_loc > 0, n_loc, 1.0), 0.0)
        sig[...] = t_val
        w_val = t_val - own * vt[cur]
        e_loc = total(w_val * w_val)
        n, s, e, c = all_reduce(n_loc, s_loc, e_loc, c_loc)
        alpha = (s + beta * c) / VEC
        diff = alpha - jnp.where(n > 0, s / jnp.where(n > 0, n, 1.0), 0.0)
        beta_new = jnp.sqrt((e + diff * n * diff) / VEC)
        alphas[pl.ds(step, 1), :] = jnp.broadcast_to(alpha, (1, LANES))
        betas[pl.ds(step, 1), :] = jnp.broadcast_to(beta_new, (1, LANES))
        inv = 1.0 / beta_new
        vt[nxt] = (sig[...] - alpha * vt[cur]) * inv
        return beta_new

    lax.fori_loop(0, NUM_STEPS, step_body, zero11)
    copies = out_start(NUM_STEPS % 3)
    out_finish(copies, NUM_STEPS % 3, NUM_STEPS).wait()


def run_kernel(psi, lw, wbig, right):
    vmem, anys = pl.BlockSpec(memory_space=pltpu.VMEM), pl.BlockSpec(memory_space=pl.ANY)
    dma = pltpu.SemaphoreType.DMA
    vm = pltpu.VMEM
    scratch = [
        vm((8, 160, 768), BF16), vm((2, 1280, 768), BF16), vm((TERMS, LANES, BOND), BF16), vm((BOND, 4096), BF16),
        vm((4, 4, 25, PAIR, LANES), BF16), vm((PAIR, 1280, LANES), BF16), vm((BOND, 4096), BF16), vm((4, 2, COLS, BOND), F32),
        vm((4, COLS, BOND), F32), vm((4, COLS, BOND), F32), vm((ROWS, BOND), F32), vm((ROWS, BOND), F32), vm((COLS, BOND), F32), vm((COLS, BOND), F32),
        vm((LANES, BOND), F32), vm((BOND, LANES), F32), vm((3, BOND, LANES), F32), vm((8, COLS, LANES), F32), vm((8, COLS, LANES), F32), vm((COLS, BOND), F32),
        vm((8, 1, LANES), F32), vm((PAIR, 1, LANES), F32),
        dma((8,)), dma((8,)), dma((4,)), dma((4,)), dma((4,)), dma((4,)), dma((8,)), dma((8,)), dma((PAIR,)), dma((PAIR,)), dma, dma,
        dma((6,)), dma((6,)), dma((8,)), dma((8,)), dma((PAIR,)), dma((PAIR,)), dma((3,)),
    ]
    return pl.pallas_call(
        kernel,
        out_shape=(jax.ShapeDtypeStruct((NUM_STEPS + 1, COLS, BOND), F32), jax.ShapeDtypeStruct((8, LANES), F32), jax.ShapeDtypeStruct((8, LANES), F32)),
        in_specs=[vmem, anys, vmem, anys],
        out_specs=(anys, vmem, vmem),
        scratch_shapes=scratch,
        compiler_params=pltpu.CompilerParams(collective_id=0, has_side_effects=True, vmem_limit_bytes=64 * 1024 * 1024 - 65536),
        name="lanczos",
    )(psi, lw, wbig, right)


def solution(mesh):
    def local_run(wave_rows, left_rows, op_pair, right_env):
        psi = wave_rows.reshape(COLS, BOND)
        left = jnp.transpose(left_rows, (1, 0, 2)).reshape(160, PAIR, ROWS)
        main = jnp.transpose(left[:, :, :32].reshape(160, PAIR, 2, PAIR), (0, 2, 1, 3)).reshape(160, 512)
        tail = jnp.broadcast_to(left[:, :, None, 32:], (160, PAIR, 2, 8)).reshape(160, 256)
        lw = jnp.concatenate([main, tail], axis=1)
        eye = jnp.eye(PAIR, dtype=bool)[None, :, None, None, :]
        wbig = jnp.where(eye, op_pair.reshape(2, PAIR, PAIR, PAIR)[..., None], jnp.zeros((), BF16)).reshape(2, 256, 256)
        vecs, alphas, betas = run_kernel(psi, lw, wbig, right_env)
        return vecs.reshape(7, 5, 4, 4, BOND), alphas[:6, 0], betas[:6, 0]

    rows = "rows"
    return jax.shard_map(local_run, mesh=mesh, in_specs=(P(rows), P(None, rows), P(), P()), out_specs=(P(None, rows), P(), P()), check_vma=False)
```

time: 1640 us -> 375 us (0.23)
  blocking collectives: 851 us -> 0 us
  waiting for transfers between devices: 385 us -> 0 us
  Pallas kernels: 0 us -> 359 us
  local copies, waits for them, and re-layouts: 197 us -> 12.8 us
  matrix products: 154 us -> 0 us
  between operations: 23.7 us -> 0.74 us
    psum x13 -> x0, blocking collectives: 851 us -> none  [global_mean(): return lax.psum(jnp.sum(local_val), row_axis) / vec_count]
    all_gather x6 -> x0, waiting for transfers between devices: 385 us -> none  [matvec(): lax.all_gather(vec_rows.astype(jnp.bfloat16), row_axis, axis=0, tiled=True)]
    pallas_call x0 -> x1, Pallas kernels: none -> 359 us  [run_kernel(): pl.pallas_call(kernel, out_shape=(jax.ShapeDtypeStruct((NUM_STEPS + 1, CO...]
    dot_general x18 -> x0, matrix products: 154 us -> none  [the longest x6 94.5 us: matvec(): jnp.dot(mid_out, right_flat, preferred_element_type=jnp.float32)]
    all_gather x5 -> x0, local copies, waits for them, and re-layouts: 112 us -> none  [matvec(): lax.all_gather(vec_rows.astype(jnp.bfloat16), row_axis, axis=0, tiled=True)]
    unnamed x59 -> x4, local copies, waits for them, and re-layouts: 40.8 us -> 0.01 us
    dot_general x6 -> x0, local copies, waits for them, and re-layouts: 18.9 us -> none  [matvec(): jnp.dot(mid_out, right_flat, preferred_element_type=jnp.float32)]
  transfers between devices with their start and end apart: 6 -> 0, of which waited for: 6 -> 0; matrix products, arithmetic and copies ran while one was open for 2% -> 0% of each run, Pallas kernels for 0% -> 0%
where the time goes in v1:
time: 375 us; the launch traced here: 374 us
  Pallas kernels  359 us (96%)
  local copies, waits for them, and re-layouts  12.8 us (3%)
    pallas_call x1, Pallas kernels, run_kernel(): pl.pallas_call(kernel, out_shape=(jax.ShapeDtypeStruct((NUM_STEPS + 1, CO...  359 us

profile of v1, /device:TPU:1, one launch (start us, length us, event | category | flops | bytes accessed | tf_op | source)
XLA Modules:
  0.0 374.3 jit_solution(14127179228955783658)
XLA Ops:
  0.6 1.9 reshape.37
  2.5 0.0 copy-start.1
  2.5 0.2 slice.17
  2.8 0.5 copy.10
  3.3 0.1 copy.12
  3.4 0.6 copy.8
  4.0 0.1 copy.11
  4.1 0.7 pad_maximum_fusion.lw
  4.9 0.0 copy-done.1
  4.9 0.2 copy.14
  5.0 1.2 broadcast_in_dim.40
  6.3 0.0 copy-start
  6.3 2.0 broadcast_in_dim.41
  8.3 0.1 broadcast_in_dim.36
  8.5 1.0 broadcast_in_dim.37
  9.5 0.7 broadcast_select_fusion.wbig
  10.2 0.0 copy-done
  10.2 0.8 reshape.36.psi
  11.0 359.3 %lanczos.1 = (f32[7,80,640]{2,1,0:T(8,128)}, f32[8,128]{1,0:T(8,128)}, f32[8,128]{1,0:T(8,128)}) custom-call(f32[80,640]{1,0:T(8,128)} %reshape.36.psi, bf16[160,768]{1,0:T(8,128)(2,1)} %pad_maximum_fusion.lw, bf16[2,256,256]{2,1,0:T(8,128)(2,1)} %broadcast_select_fusion.wbig, bf16[32,640,640]{2,1,0:T(8,128)(2,1)} %right.1), custom_call_target="tpu_custom_call" | custom-call | tf_op jit(solution)/shard_map/lanczos/pallas_call | solution.py:418
  370.3 1.4 slice_reduce_fusion
  371.7 2.7 reshape.41
  (3 shorter events, 0.0 us)
Async XLA Ops:
  2.5 2.3 copy-start.1
  6.3 3.9 %copy-start = (f32[5,4,4,640]{3,2,1,0:T(4,128)S(1)}, f32[5,4,4,640]{3,2,1,0:T(4,128)}, u32[]{:S(2)}) copy-start(f32[5,4,4,640]{3,2,1,0:T(4,128)} %param.4) | copy-start | bytes 614404

commit v2 on v0

v2 whole, which is shorter than its diff:
```python
import functools

import jax
import jax.numpy as jnp
from jax import lax
from jax.experimental import pallas as pl
from jax.experimental.pallas import tpu as pltpu
from jax.sharding import PartitionSpec as P

NUM_STEPS = 6
MESH = pl.DeviceIdType.MESH
F32 = jnp.float32
BF16 = jnp.bfloat16

ROWS, COLS = 40, 80
BOND, PAIR, TERMS = 640, 16, 32
LANES = 128
VEC = BOND * BOND * PAIR


def remote(src, dst, send, recv, dev):
    return pltpu.make_async_remote_copy(src_ref=src, dst_ref=dst, send_sem=send, recv_sem=recv, device_id=(dev,), device_id_type=MESH)


def lane_roll(val, shift):
    shift = shift % LANES
    return val if shift == 0 else pltpu.roll(val, shift, axis=val.ndim - 1)


def lane_iota(val):
    return lax.broadcasted_iota(jnp.int32, val.shape, val.ndim - 1)


def take_piece(tiles, idx):
    tile, off = divmod(COLS * idx, LANES)
    out = lane_roll(tiles(tile), -off)
    lane = lane_iota(out)
    if off + COLS > LANES:
        out = jnp.where(lane < LANES - off, out, lane_roll(tiles(tile + 1), -off))
    return jnp.where(lane < COLS, out, jnp.zeros_like(out))


def dense_tile(pieces, tile):
    out = None
    for idx in range(8):
        shift = COLS * idx - LANES * tile
        if shift <= -COLS or shift >= LANES:
            continue
        moved = lane_roll(pieces(idx), shift)
        out = moved if out is None else jnp.where(lane_iota(moved) >= shift, moved, out)
    return out


def kernel(psi, left, pair, right, vecs, alphas, betas, lall, lh, wbig, rtmp, rt, ug, xs, ys, part, rd, ssum, ra, rb, fl, fr, fin,
           sig, vt, piece_buf, out_recv, outv, ar1, ar2, psi_s, psi_r, l_s, l_r, out_s, out_r, g_s, g_r, d_s, d_r,
           ring_s, ring_r, a1_s, a1_r, a2_s, a2_r, loc):
    me = lax.axis_index("rows")
    core = lax.rem(me, 2)
    x = lax.rem(me // 2, 4)
    y = lax.rem(me // 8, 4)
    z = me // 32
    i = me // 8
    j = lax.rem(me, 8)
    lo, hi = pl.ds(0, ROWS), pl.ds(ROWS, ROWS)

    def wrap4(val):
        return lax.rem(val + 4, 4)

    def in_row(dj):
        jj = lax.rem(j + dj, 8)
        return jj, i * 8 + jj

    def in_col(di):
        ii = lax.rem(i + di, PAIR)
        return ii, ii * 8 + j

    def rows_of(jj):
        return pl.ds(pl.multiple_of(jj * COLS, COLS), COLS)

    barrier = pltpu.get_barrier_semaphore()
    for dj in range(1, 8):
        pl.semaphore_signal(barrier, inc=1, device_id=(in_row(dj)[1],), device_id_type=MESH)
    for di in range(1, PAIR):
        pl.semaphore_signal(barrier, inc=1, device_id=(in_col(di)[1],), device_id_type=MESH)
    pl.semaphore_wait(barrier, 22)

    partner = me + 1 - 2 * core
    x_up, x_dn = i * 8 + wrap4(x + 1) * 2 + core, i * 8 + wrap4(x - 1) * 2 + core
    my_rows = rows_of(j)

    cp_r = pltpu.make_async_copy(right.at[:, my_rows, :], rtmp.at[:, pl.ds(0, COLS), :], loc.at[0])
    cp_r.start()
    cp_l = pltpu.make_async_copy(left, lall.at[x, core], loc.at[1])
    cp_l.start()

    row_lane = lax.broadcasted_iota(jnp.int32, (1, LANES), 1)

    def total(val):
        return jnp.sum(jnp.sum(val, axis=0, keepdims=True), axis=1, keepdims=True)

    def ratio(num, den):
        good = den > 0
        return jnp.where(good, num / jnp.where(good, den, 1.0), 0.0)

    def pack_row(stats):
        row = jnp.zeros((1, LANES), F32)
        for idx, val in enumerate(stats):
            row = jnp.where(row_lane == idx, val, row)
        return row

    def merge(mat):
        lane = lax.broadcasted_iota(jnp.int32, mat.shape, 2)
        n, s, e, c = (jnp.sum(jnp.where(lane == idx, mat, 0.0), axis=2, keepdims=True) for idx in range(4))
        n_all, s_all, c_all = (jnp.sum(val, axis=0, keepdims=True) for val in (n, s, c))
        diff = ratio(s, n) - ratio(s_all, n_all)
        e_all = jnp.sum(e + diff * n * diff, axis=0, keepdims=True)
        return tuple(val.reshape(1, 1) for val in (n_all, s_all, e_all, c_all))

    def all_reduce(stats, first=None, second=None):
        ar1[j] = pack_row(stats)
        copies = []
        for dj in range(1, 8):
            jj, dev = in_row(dj)
            cp = remote(ar1.at[j], ar1.at[j], a1_s.at[jj], a1_r.at[j], dev)
            cp.start()
            copies.append(cp)
        if first:
            first()
        for dj in range(1, 8):
            jj, dev = in_row(dj)
            remote(ar1.at[jj], ar1.at[jj], a1_s.at[jj], a1_r.at[jj], dev).wait_recv()
        ar2[i] = pack_row(merge(ar1[...]))
        for di in range(1, PAIR):
            ii, dev = in_col(di)
            cp = remote(ar2.at[i], ar2.at[i], a2_s.at[ii], a2_r.at[i], dev)
            cp.start()
            copies.append(cp)
        if second:
            second()
        for di in range(1, PAIR):
            ii, dev = in_col(di)
            remote(ar2.at[ii], ar2.at[ii], a2_s.at[ii], a2_r.at[ii], dev).wait_recv()
        for cp in copies:
            cp.wait_send()
        return merge(ar2[...])

    def l_copy(src, rows, idx, dev):
        ref = lall.at[src[0], src[1], rows]
        return remote(ref, ref, l_s.at[idx], l_r.at[idx], dev)

    every, low, high = pl.ds(0, 160), pl.ds(0, COLS), pl.ds(COLS, COLS)

    def psi_sends():
        for jj in range(8):
            piece_buf[jj] = take_piece(lambda t: psi[:, LANES * t:LANES * t + LANES], jj)
        vt[0, my_rows, :] = piece_buf[j]
        for dj in range(1, 8):
            jj, dev = in_row(dj)
            remote(piece_buf.at[jj], vt.at[0, my_rows], psi_s.at[jj], psi_r.at[j], dev).start()
        cp_l.wait()
        l_copy((x, core), every, 0, x_up).start()
        l_copy((x, core), every, 1, x_dn).start()
        l_copy((x, core), every, 4, partner).start()
        spread = jnp.where(lax.broadcasted_iota(jnp.int32, (PAIR, 256), 1) // PAIR == lax.broadcasted_iota(jnp.int32, (PAIR, 256), 0), 1.0, 0.0).astype(BF16)
        same = lax.broadcasted_iota(jnp.int32, (256, 256), 1) % PAIR == lax.broadcasted_iota(jnp.int32, (256, 256), 0) // PAIR
        for h in range(2):
            wide = jnp.dot(pair[pl.ds(256 * h, 256), :], spread, preferred_element_type=F32)
            wbig[h] = jnp.where(same, wide, 0.0).astype(BF16)
        vt[2] = jnp.zeros((BOND, LANES), F32)
        fin[...] = jnp.zeros((LANES, BOND), F32)

    def turn_right():
        cp_r.wait()

        def body(k, carry):
            rtmp[k, pl.ds(COLS, 48), :] = jnp.zeros((48, BOND), BF16)
            for b in range(5):
                rt[pl.ds(LANES * b, LANES), pl.ds(pl.multiple_of(k * LANES, LANES), LANES)] = rtmp[k, :, pl.ds(LANES * b, LANES)].T
            return carry

        lax.fori_loop(0, TERMS, body, 0)

    psi_val = psi[...]
    n_psi = all_reduce([total(psi_val * psi_val)], psi_sends, turn_right)[0]
    inv_norm = 1.0 / jnp.sqrt(n_psi / VEC)

    for dj in range(1, 8):
        jj, dev = in_row(dj)
        cp = remote(piece_buf.at[jj], vt.at[0, rows_of(jj)], psi_s.at[jj], psi_r.at[jj], dev)
        cp.wait_recv()
        cp.wait_send()
    vt[0] = vt[0] * inv_norm
    outv[...] = psi_val * inv_norm
    cp_v = pltpu.make_async_copy(outv, vecs.at[0], loc.at[2])
    cp_v.start()

    lower, upper, far = (wrap4(x - 1), core), (wrap4(x + 1), core), (wrap4(x + 2), core)

    def left_forward():
        l_copy(lower, every, 0, x_up).wait_recv()
        l_copy(lower, low, 2, x_up).start()
        l_copy(upper, every, 1, x_dn).wait_recv()
        l_copy(upper, high, 3, x_dn).start()
        l_copy(lower, every, 5, partner).start()
        l_copy(upper, every, 6, partner).start()

    def left_finish():
        l_copy(far, low, 2, x_up).wait_recv()
        l_copy(far, high, 3, x_dn).wait_recv()
        l_copy(far, every, 7, partner).start()
        for idx, dx in ((4, 0), (5, 3), (6, 1), (7, 2)):
            l_copy((wrap4(x + dx), 1 - core), every, idx, partner).wait_recv()
        for idx, rows in enumerate((every, every, low, high, every, every, every, every)):
            l_copy((x, core), rows, idx, partner).wait_send()
        for h in range(2):
            src = lax.broadcasted_iota(jnp.int32, (BOND, 768), 0)
            col = lax.broadcasted_iota(jnp.int32, (BOND, 768), 1)
            group = (col % 256) // PAIR
            main = ROWS * group + PAIR * (col // 256) + col % PAIR
            tail = jnp.where((col // 8) % 2 == h, ROWS * group + 32 + col % 8, -1)
            order = jnp.where(src == jnp.where(col < 512, main, tail), 1.0, 0.0).astype(BF16)

            def body(t, carry):
                rows = pl.ds(pl.multiple_of(t * 160, 160), 160)
                lh[h, rows, :] = jnp.dot(lall[t // 2, t % 2], order, preferred_element_type=F32).astype(BF16)
                return carry

            lax.fori_loop(0, 8, body, 0)

    def flow(base, firsts, seconds, ref, parts):
        done = []
        offs = (0, -1, 1, 2)

        def send(blk, prt, idx, dev):
            here = ref(blk, parts[prt])
            cp = remote(here, here, g_s.at[base + idx], g_r.at[base + idx], dev)
            cp.start()
            done.append(cp)

        def wait(blk, prt, idx):
            here = ref(blk, parts[prt])
            remote(here, here, g_s.at[base + idx], g_r.at[base + idx], partner).wait_recv()

        def second(b, prt):
            for way in ((0, 1) if prt == 0 else (1, 0)):
                send((offs[b], 0), prt, 6 * b + 6 + 2 * way + prt, seconds[way])

        def second_forward(b):
            wait((offs[b], -1), 0, 6 * b + 6)
            send((offs[b], -1), 0, 6 * b + 10, seconds[0])
            wait((offs[b], 1), 1, 6 * b + 9)
            send((offs[b], 1), 1, 6 * b + 11, seconds[1])

        for prt, way in ((0, 0), (1, 1), (1, 0), (0, 1)):
            send((0, 0), prt, 2 * way + prt, firsts[way])
        yield
        second(0, 0)
        second(0, 1)
        yield
        wait((-1, 0), 0, 0)
        send((-1, 0), 0, 4, firsts[0])
        second(1, 0)
        yield
        wait((1, 0), 1, 3)
        send((1, 0), 1, 5, firsts[1])
        second(2, 1)
        yield
        wait((-1, 0), 1, 1)
        second(1, 1)
        wait((1, 0), 0, 2)
        second(2, 0)
        yield
        second_forward(0)
        yield
        wait((2, 0), 0, 4)
        second(3, 0)
        wait((2, 0), 1, 5)
        second(3, 1)
        yield
        for b in range(1, 4):
            second_forward(b)
            yield
        for b in range(4):
            for off, prt, idx in ((-1, 1, 7), (1, 0, 8), (2, 0, 10), (2, 1, 11)):
                wait((offs[b], off), prt, 6 * b + idx)
        for cp in done:
            cp.wait_send()
        yield

    def device(zz, yy):
        return (wrap4(zz) * 4 + wrap4(yy)) * 8 + j

    y_ways, z_ways = (device(z, y + 1), device(z, y - 1)), (device(z + 1, y), device(z - 1, y))

    def gather(busy):
        def y_first(blk, prt):
            return ug.at[wrap4(z + blk[1]), wrap4(y + blk[0]), pl.ds(*prt)]

        def z_first(blk, prt):
            return ug.at[wrap4(z + blk[0]), wrap4(y + blk[1]), pl.ds(*prt)]

        both = [flow(0, y_ways, z_ways, y_first, ((0, 6), (6, 6))), flow(30, z_ways, y_ways, z_first, ((12, 6), (18, 7)))]
        for idx, unused in enumerate(zip(*both)):
            if idx == 1:
                busy()

    def out_copy(slot, jj, dev):
        return remote(sig.at[rows_of(jj)], out_recv.at[slot], out_s.at[jj], out_r.at[slot], dev)

    def out_start():
        for dj in range(1, 8):
            jj, dev = in_row(dj)
            out_copy(j, jj, dev).start()
        out_recv[j] = sig[my_rows, :]

    def out_finish(step):
        for dj in range(1, 8):
            jj, dev = in_row(dj)
            out_copy(jj, jj, dev).wait_recv()
            out_copy(j, jj, dev).wait_send()
        cp_v.wait()
        alpha, inv = fin[pl.ds(COLS, 1), pl.ds(0, 1)], fin[pl.ds(COLS + 8, 1), pl.ds(0, 1)]
        for tile in range(5):
            lanes = pl.ds(LANES * tile, LANES)
            outv[:, lanes] = (dense_tile(lambda idx: out_recv[idx], tile) - alpha * outv[:, lanes]) * inv
        pltpu.make_async_copy(outv, vecs.at[step], loc.at[2]).start()

    def step_body(step, beta):
        cur = lax.rem(step, 3)
        prev = lax.rem(step + 2, 3)
        nxt = lax.rem(step + 1, 3)

        with jax.named_scope("pack"):
            strided = [vt[cur, pl.ds(r, ROWS, stride=PAIR), :] for r in range(PAIR)]
            for lt in range(5):
                half = [dense_tile(lambda idx, h=h: strided[8 * h + idx], lt) for h in range(2)]
                for h in range(2):
                    for tt in range(2):
                        ug[z, y, lt * 5 + 2 * h + tt] = half[h][PAIR * tt:PAIR * tt + PAIR].astype(BF16)
                ug[z, y, lt * 5 + 4] = jnp.concatenate([half[0][32:ROWS], half[1][32:ROWS]], axis=0).astype(BF16)

        def busy():
            @pl.when(step == 0)
            def _():
                left_forward()

            @pl.when(step > 0)
            def _():
                out_finish(step)

        with jax.named_scope("gather"):
            gather(busy)

        @pl.when(step == 0)
        def _():
            with jax.named_scope("leftfin"):
                left_finish()

        def left_half(h, carry):
            for rp in range(4):
                cols = []
                for rr in range(2):
                    idx = 2 * rp + rr
                    rows = [take_piece(lambda t, tr=tr: ug[:, :, t * 5 + tr].reshape(256, LANES), idx) for tr in (2 * h, 2 * h + 1, 4)]
                    cols.append(jnp.concatenate(rows, axis=0))
                rhs = jnp.concatenate(cols, axis=1)
                for mc in range(2):
                    rows = pl.ds(BOND * mc, BOND)
                    res = jnp.dot(lh[h, rows, :], rhs, preferred_element_type=F32).astype(BF16)
                    for rr in range(2):
                        xs[h * 8 + 2 * rp + rr, rows, :] = res[:, LANES * rr:LANES * rr + LANES]
            return carry

        with jax.named_scope("lstage"):
            lax.fori_loop(0, 2, left_half, 0)

        def some_rows(ap, carry):
            for pr in range(4):
                for h in range(2):
                    starts = [pl.multiple_of((ap * 8 + 2 * pr + aa) * 32 + PAIR * h, PAIR) for aa in range(2)]
                    rhs = jnp.concatenate([xs[:, pl.ds(start, PAIR), :].reshape(256, LANES) for start in starts], axis=1)
                    res = jnp.dot(wbig[h], rhs, preferred_element_type=F32).astype(BF16)
                    for aa in range(2):
                        rows = pl.ds(pl.multiple_of((ap * 8 + 2 * pr + aa) * PAIR, PAIR), PAIR)
                        for k in range(PAIR):
                            ys[rows, pl.ds((PAIR * h + k) * LANES, LANES)] = res[PAIR * k:PAIR * k + PAIR, LANES * aa:LANES * aa + LANES]
            return carry

        with jax.named_scope("wstage"):
            lax.fori_loop(0, 5, some_rows, 0)

        spots = [wrap4(x + dx) for dx in (2, 1, 3, 0)]

        def sigma(first, cols):
            lhs = jnp.concatenate([rt[pl.ds(pl.multiple_of(spot * 160, 160), 160), :] for spot in spots[first:first + 2]], axis=0)
            res = lax.dot_general(lhs, ys[cols, :], (((1,), (1,)), ((), ())), preferred_element_type=F32)
            for idx in range(4):
                part[first + idx // 2, idx % 2, :, cols] = res[idx * COLS:idx * COLS + COLS]

        def swap(first):
            return remote(part.at[pl.ds(first, 2), 1 - core], rd.at[pl.ds(first, 2)], d_s.at[first // 2], d_r.at[first // 2], partner)

        def add_pair(first):
            swap(first).wait()
            for slot in (first, first + 1):
                ssum[slot] = part[slot, core] + rd[slot]

        def ring(slot, rows, dst, idx, dev):
            return remote(ssum.at[slot, rows], dst, ring_s.at[idx], ring_r.at[idx], dev)

        copies = [ring(0, lo, ra, 0, x_up), ring(0, hi, rb, 1, x_dn), ring(1, hi, fl.at[hi], 2, x_up), ring(2, lo, fr.at[lo], 3, x_dn),
                  ring(1, lo, fl.at[lo], 4, x_up), ring(2, hi, fr.at[hi], 5, x_dn)]
        with jax.named_scope("rstage"):
            sigma(0, pl.ds(0, BOND))
            swap(0).start()
            sigma(2, pl.ds(0, 384))
        with jax.named_scope("ring0"):
            add_pair(0)
            for cp in copies[:3]:
                cp.start()
        with jax.named_scope("rstage2"):
            sigma(2, pl.ds(384, 256))
            swap(2).start()
        with jax.named_scope("xring"):
            add_pair(2)
            copies[3].start()
            copies[0].wait_recv()
            ssum[1, lo] = ssum[1, lo] + ra[...]
            copies[4].start()
            copies[1].wait_recv()
            ssum[2, hi] = ssum[2, hi] + rb[...]
            copies[5].start()
            v_cur = vt[cur]
            n_loc = total(v_cur * v_cur)
            c_loc = total(v_cur * vt[prev])
            for cp in copies[2:]:
                cp.wait_recv()
            fin[pl.ds(0, COLS), :] = ssum[3] + fl[...] + fr[...]
            for cp in copies:
                cp.wait_send()
        with jax.named_scope("turn"):
            for b in range(5):
                rows = pl.ds(LANES * b, LANES)
                sig[rows, :] = jnp.where(row_lane < COLS, fin[:, rows].T, 0.0)

        with jax.named_scope("vec1"):
            t_val = sig[...] - beta * vt[prev]
            s_loc = total(t_val * vt[cur])
            sig[...] = t_val
            w_val = t_val - ratio(s_loc, n_loc) * vt[cur]
            e_loc = total(w_val * w_val)
        with jax.named_scope("allred"):
            n, s, e, c = all_reduce([n_loc, s_loc, e_loc, c_loc], out_start)
        with jax.named_scope("vec2"):
            alpha = (s + beta * c) / VEC
            diff = alpha - ratio(s, n)
            beta_new = jnp.sqrt((e + diff * n * diff) / VEC)
            inv = 1.0 / beta_new
            vt[nxt] = (sig[...] - alpha * vt[cur]) * inv
            fin[pl.ds(COLS, 1), :] = jnp.broadcast_to(alpha, (1, BOND))
            fin[pl.ds(COLS + 8, 1), :] = jnp.broadcast_to(inv, (1, BOND))
            alphas[step] = alpha[0, 0]
            betas[step] = beta_new[0, 0]
        return beta_new

    lax.fori_loop(0, NUM_STEPS, step_body, jnp.zeros((1, 1), F32))
    out_finish(NUM_STEPS)
    cp_v.wait()


def run_kernel(psi, left, pair, right):
    vmem, anys, smem = (pl.BlockSpec(memory_space=space) for space in (pltpu.VMEM, pl.ANY, pltpu.SMEM))
    dma = pltpu.SemaphoreType.DMA
    vm = pltpu.VMEM
    block = (COLS, BOND)
    scratch = [
        vm((4, 2, 160, BOND), BF16), vm((2, 1280, 768), BF16), vm((2, 256, 256), BF16), vm((TERMS, LANES, BOND), BF16), vm((BOND, 4096), BF16),
        vm((4, 4, 25, PAIR, LANES), BF16), vm((PAIR, 1280, LANES), BF16), vm((BOND, 4096), BF16), vm((4, 2) + block, F32),
        vm((4,) + block, F32), vm((4,) + block, F32), vm((ROWS, BOND), F32), vm((ROWS, BOND), F32), vm(block, F32), vm(block, F32),
        vm((LANES, BOND), F32), vm((BOND, LANES), F32), vm((3, BOND, LANES), F32), vm((8, COLS, LANES), F32), vm((8, COLS, LANES), F32), vm(block, F32),
        vm((8, 1, LANES), F32), vm((PAIR, 1, LANES), F32),
    ] + [dma((num,)) for num in (8, 8, 8, 8, 8, 8, 60, 60, 2, 2, 6, 6, 8, 8, PAIR, PAIR, 3)]
    scal = jax.ShapeDtypeStruct((NUM_STEPS,), F32)
    return pl.pallas_call(
        kernel,
        out_shape=(jax.ShapeDtypeStruct((NUM_STEPS + 1,) + block, F32), scal, scal),
        in_specs=[vmem, anys, vmem, anys],
        out_specs=(anys, smem, smem),
        scratch_shapes=scratch,
        compiler_params=pltpu.CompilerParams(collective_id=0, has_side_effects=True, vmem_limit_bytes=67043328),
        name="lanczos",
    )(psi, left, pair, right)


def solution(mesh):
    def local_run(wave_rows, left_rows, op_pair, right_env):
        psi = wave_rows.reshape(COLS, BOND)
        left = jnp.transpose(left_rows, (1, 0, 2)).reshape(160, BOND)
        vecs, alphas, betas = run_kernel(psi, left, op_pair.reshape(512, PAIR), right_env)
        return vecs.reshape(7, 5, 4, 4, BOND), alphas, betas

    rows = "rows"
    return jax.shard_map(local_run, mesh=mesh, in_specs=(P(rows), P(None, rows), P(), P()), out_specs=(P(None, rows), P(), P()), check_vma=False)
```

time: 1640 us -> 310 us (0.19)
  blocking collectives: 851 us -> 0 us
  waiting for transfers between devices: 385 us -> 0 us
  Pallas kernels: 0 us -> 302 us
  local copies, waits for them, and re-layouts: 197 us -> 7 us
  matrix products: 154 us -> 0 us
  between operations: 23.7 us -> 0.66 us
    psum x13 -> x0, blocking collectives: 851 us -> none  [global_mean(): return lax.psum(jnp.sum(local_val), row_axis) / vec_count]
    all_gather x6 -> x0, waiting for transfers between devices: 385 us -> none  [matvec(): lax.all_gather(vec_rows.astype(jnp.bfloat16), row_axis, axis=0, tiled=True)]
    pallas_call x0 -> x1, Pallas kernels: none -> 302 us  [run_kernel(): pl.pallas_call(kernel, out_shape=(jax.ShapeDtypeStruct((NUM_STEPS + 1,) +...]
    dot_general x18 -> x0, matrix products: 154 us -> none  [the longest x6 94.5 us: matvec(): jnp.dot(mid_out, right_flat, preferred_element_type=jnp.float32)]
    all_gather x5 -> x0, local copies, waits for them, and re-layouts: 112 us -> none  [matvec(): lax.all_gather(vec_rows.astype(jnp.bfloat16), row_axis, axis=0, tiled=True)]
    unnamed x59 -> x7, local copies, waits for them, and re-layouts: 40.8 us -> 2.66 us
    dot_general x6 -> x0, local copies, waits for them, and re-layouts: 18.9 us -> none  [matvec(): jnp.dot(mid_out, right_flat, preferred_element_type=jnp.float32)]
  transfers between devices with their start and end apart: 6 -> 0, of which waited for: 6 -> 0; matrix products, arithmetic and copies ran while one was open for 2% -> 0% of each run, Pallas kernels for 0% -> 0%
where the time goes in v2:
time: 310 us; the launch traced here: 309 us
  Pallas kernels  302 us (97%)
  local copies, waits for them, and re-layouts  7 us (2%)
    pallas_call x1, Pallas kernels, run_kernel(): pl.pallas_call(kernel, out_shape=(jax.ShapeDtypeStruct((NUM_STEPS + 1,) +...  302 us

profile of v2, /device:TPU:1, one launch (start us, length us, event | category | flops | bytes accessed | tf_op | source)
XLA Modules:
  0.0 309.2 jit_solution(14584363077615707362)
XLA Ops:
  0.6 1.6 copy.7
  2.3 1.7 reshape.18.psi
  3.9 301.5 %lanczos.1 = (f32[7,80,640]{2,1,0:T(8,128)}, f32[6]{0:T(128)}, f32[6]{0:T(128)}) custom-call(f32[80,640]{1,0:T(8,128)} %reshape.18.psi, bf16[160,640]{1,0:T(8,128)(2,1)} %bitcast.5, bf16[512,16]{1,0:T(8,128)(2,1)} %bitcast.4, bf16[32,640,640]{2,1,0:T(8,128)(2,1)} %right.1), custom_call_target="tpu_custom_call" | custom-call | tf_op jit(solution)/shard_map/lanczos/pallas_call | solution.py:484
  305.5 0.0 copy-start.1
  305.5 0.0 copy-start
  305.5 2.7 reshape.21
  308.2 0.0 copy-done.1
  308.2 0.5 copy.10
  308.7 0.0 copy-done
  308.7 0.5 copy.11
Async XLA Ops:
  305.5 2.7 copy-start.1
  305.5 3.2 %copy-start = (f32[6]{0:T(128)S(1)}, f32[6]{0:T(128)}, u32[]{:S(2)}) copy-start(f32[6]{0:T(128)} %get-tuple-element.14) | copy-start | bytes 76

commit v3 on v2

--- a/solution.py
+++ b/solution.py
@@ -52,8 +52,8 @@
 
 
 def kernel(psi, left, pair, right, vecs, alphas, betas, lall, lh, wbig, rtmp, rt, ug, xs, ys, part, rd, ssum, ra, rb, fl, fr, fin,
-           sig, vt, piece_buf, out_recv, outv, ar1, ar2, psi_s, psi_r, l_s, l_r, out_s, out_r, g_s, g_r, d_s, d_r,
-           ring_s, ring_r, a1_s, a1_r, a2_s, a2_r, loc):
+           sig, vt, piece_buf, out_recv, outv, stat, psi_s, psi_r, l_s, l_r, out_s, out_r, g_s, g_r, d_s, d_r,
+           ring_s, ring_r, a_s, a_r, loc):
     me = lax.axis_index("rows")
     core = lax.rem(me, 2)
     x = lax.rem(me // 2, 4)
@@ -70,19 +70,17 @@
         jj = lax.rem(j + dj, 8)
         return jj, i * 8 + jj
 
-    def in_col(di):
-        ii = lax.rem(i + di, PAIR)
-        return ii, ii * 8 + j
-
     def rows_of(jj):
         return pl.ds(pl.multiple_of(jj * COLS, COLS), COLS)
 
     barrier = pltpu.get_barrier_semaphore()
-    for dj in range(1, 8):
-        pl.semaphore_signal(barrier, inc=1, device_id=(in_row(dj)[1],), device_id_type=MESH)
-    for di in range(1, PAIR):
-        pl.semaphore_signal(barrier, inc=1, device_id=(in_col(di)[1],), device_id_type=MESH)
-    pl.semaphore_wait(barrier, 22)
+
+    def greet(d, carry):
+        pl.semaphore_signal(barrier, inc=1, device_id=(lax.rem(me + d, LANES),), device_id_type=MESH)
+        return carry
+
+    lax.fori_loop(1, LANES, greet, 0)
+    pl.semaphore_wait(barrier, LANES - 1)
 
     partner = me + 1 - 2 * core
     x_up, x_dn = i * 8 + wrap4(x + 1) * 2 + core, i * 8 + wrap4(x - 1) * 2 + core
@@ -102,47 +100,28 @@
         good = den > 0
         return jnp.where(good, num / jnp.where(good, den, 1.0), 0.0)
 
-    def pack_row(stats):
+    def all_reduce(stats, hook):
         row = jnp.zeros((1, LANES), F32)
         for idx, val in enumerate(stats):
             row = jnp.where(row_lane == idx, val, row)
-        return row
-
-    def merge(mat):
-        lane = lax.broadcasted_iota(jnp.int32, mat.shape, 2)
-        n, s, e, c = (jnp.sum(jnp.where(lane == idx, mat, 0.0), axis=2, keepdims=True) for idx in range(4))
-        n_all, s_all, c_all = (jnp.sum(val, axis=0, keepdims=True) for val in (n, s, c))
-        diff = ratio(s, n) - ratio(s_all, n_all)
-        e_all = jnp.sum(e + diff * n * diff, axis=0, keepdims=True)
-        return tuple(val.reshape(1, 1) for val in (n_all, s_all, e_all, c_all))
-
-    def all_reduce(stats, first=None, second=None):
-        ar1[j] = pack_row(stats)
-        copies = []
-        for dj in range(1, 8):
-            jj, dev = in_row(dj)
-            cp = remote(ar1.at[j], ar1.at[j], a1_s.at[jj], a1_r.at[j], dev)
-            cp.start()
-            copies.append(cp)
-        if first:
-            first()
-        for dj in range(1, 8):
-            jj, dev = in_row(dj)
-            remote(ar1.at[jj], ar1.at[jj], a1_s.at[jj], a1_r.at[jj], dev).wait_recv()
-        ar2[i] = pack_row(merge(ar1[...]))
-        for di in range(1, PAIR):
-            ii, dev = in_col(di)
-            cp = remote(ar2.at[i], ar2.at[i], a2_s.at[ii], a2_r.at[i], dev)
-            cp.start()
-            copies.append(cp)
-        if second:
-            second()
-        for di in range(1, PAIR):
-            ii, dev = in_col(di)
-            remote(ar2.at[ii], ar2.at[ii], a2_s.at[ii], a2_r.at[ii], dev).wait_recv()
-        for cp in copies:
-            cp.wait_send()
-        return merge(ar2[...])
+        stat[me, pl.ds(0, 1), :] = row
+        stat[me, pl.ds(1, 1), :] = jnp.broadcast_to(ratio(stats[1], stats[0]), (1, LANES))
+
+        def give(d, carry):
+            dev = lax.rem(me + d, LANES)
+            remote(stat.at[me], stat.at[me], a_s, a_r, dev).start()
+            return carry
+
+        lax.fori_loop(1, LANES, give, 0, unroll=True)
+        hook()
+        most = stat.at[pl.ds(0, LANES - 1)]
+        remote(most, most, a_s, a_r, partner).wait()
+        rows = stat[:, pl.ds(0, 1), :]
+        sums = jnp.sum(rows, axis=0)
+        n, s, e, c = (jnp.sum(jnp.where(row_lane == idx, sums, 0.0), axis=1, keepdims=True) for idx in range(4))
+        diff = stat[:, pl.ds(1, 1), :] - ratio(s, n)[None]
+        moved = jnp.sum(diff * rows * diff, axis=0)
+        return n, s, e + jnp.sum(jnp.where(row_lane == 0, moved, 0.0), axis=1, keepdims=True), c
 
     def l_copy(src, rows, idx, dev):
         ref = lall.at[src[0], src[1], rows]
@@ -180,8 +159,24 @@
 
         lax.fori_loop(0, TERMS, body, 0)
 
+    lower, upper, far = (wrap4(x - 1), core), (wrap4(x + 1), core), (wrap4(x + 2), core)
+
+    def left_forward():
+        l_copy(lower, every, 0, x_up).wait_recv()
+        l_copy(lower, low, 2, x_up).start()
+        l_copy(upper, every, 1, x_dn).wait_recv()
+        l_copy(upper, high, 3, x_dn).start()
+        l_copy(lower, every, 5, partner).start()
+        l_copy(upper, every, 6, partner).start()
+
+    def start_up():
+        psi_sends()
+        turn_right()
+        left_forward()
+
     psi_val = psi[...]
-    n_psi = all_reduce([total(psi_val * psi_val)], psi_sends, turn_right)[0]
+    zero = jnp.zeros((1, 1), F32)
+    n_psi = all_reduce([total(psi_val * psi_val), zero], start_up)[0]
     inv_norm = 1.0 / jnp.sqrt(n_psi / VEC)
 
     for dj in range(1, 8):
@@ -193,16 +188,6 @@
     outv[...] = psi_val * inv_norm
     cp_v = pltpu.make_async_copy(outv, vecs.at[0], loc.at[2])
     cp_v.start()
-
-    lower, upper, far = (wrap4(x - 1), core), (wrap4(x + 1), core), (wrap4(x + 2), core)
-
-    def left_forward():
-        l_copy(lower, every, 0, x_up).wait_recv()
-        l_copy(lower, low, 2, x_up).start()
-        l_copy(upper, every, 1, x_dn).wait_recv()
-        l_copy(upper, high, 3, x_dn).start()
-        l_copy(lower, every, 5, partner).start()
-        l_copy(upper, every, 6, partner).start()
 
     def left_finish():
         l_copy(far, low, 2, x_up).wait_recv()
@@ -253,16 +238,16 @@
 
         for prt, way in ((0, 0), (1, 1), (1, 0), (0, 1)):
             send((0, 0), prt, 2 * way + prt, firsts[way])
+        for prt in range(2):
+            send((0, 0), prt, 4 + prt, firsts[2])
         yield
         second(0, 0)
         second(0, 1)
         yield
         wait((-1, 0), 0, 0)
-        send((-1, 0), 0, 4, firsts[0])
         second(1, 0)
         yield
         wait((1, 0), 1, 3)
-        send((1, 0), 1, 5, firsts[1])
         second(2, 1)
         yield
         wait((-1, 0), 1, 1)
@@ -290,7 +275,7 @@
     def device(zz, yy):
         return (wrap4(zz) * 4 + wrap4(yy)) * 8 + j
 
-    y_ways, z_ways = (device(z, y + 1), device(z, y - 1)), (device(z + 1, y), device(z - 1, y))
+    y_ways, z_ways = (device(z, y + 1), device(z, y - 1), device(z, y + 2)), (device(z + 1, y), device(z - 1, y), device(z + 2, y))
 
     def gather(busy):
         def y_first(blk, prt):
@@ -301,8 +286,8 @@
 
         both = [flow(0, y_ways, z_ways, y_first, ((0, 6), (6, 6))), flow(30, z_ways, y_ways, z_first, ((12, 6), (18, 7)))]
         for idx, unused in enumerate(zip(*both)):
-            if idx == 1:
-                busy()
+            if idx in busy:
+                busy[idx]()
 
     def out_copy(slot, jj, dev):
         return remote(sig.at[rows_of(jj)], out_recv.at[slot], out_s.at[jj], out_r.at[slot], dev)
@@ -339,22 +324,18 @@
                         ug[z, y, lt * 5 + 2 * h + tt] = half[h][PAIR * tt:PAIR * tt + PAIR].astype(BF16)
                 ug[z, y, lt * 5 + 4] = jnp.concatenate([half[0][32:ROWS], half[1][32:ROWS]], axis=0).astype(BF16)
 
-        def busy():
+        def first_step():
             @pl.when(step == 0)
             def _():
-                left_forward()
-
+                left_finish()
+
+        def later_step():
             @pl.when(step > 0)
             def _():
                 out_finish(step)
 
         with jax.named_scope("gather"):
-            gather(busy)
-
-        @pl.when(step == 0)
-        def _():
-            with jax.named_scope("leftfin"):
-                left_finish()
+            gather({1: first_step, 6: later_step})
 
         def left_half(h, carry):
             for rp in range(4):
@@ -386,58 +367,83 @@
                             ys[rows, pl.ds((PAIR * h + k) * LANES, LANES)] = res[PAIR * k:PAIR * k + PAIR, LANES * aa:LANES * aa + LANES]
             return carry
 
-        with jax.named_scope("wstage"):
-            lax.fori_loop(0, 5, some_rows, 0)
-
-        spots = [wrap4(x + dx) for dx in (2, 1, 3, 0)]
-
-        def sigma(first, cols):
-            lhs = jnp.concatenate([rt[pl.ds(pl.multiple_of(spot * 160, 160), 160), :] for spot in spots[first:first + 2]], axis=0)
-            res = lax.dot_general(lhs, ys[cols, :], (((1,), (1,)), ((), ())), preferred_element_type=F32)
-            for idx in range(4):
-                part[first + idx // 2, idx % 2, :, cols] = res[idx * COLS:idx * COLS + COLS]
-
-        def swap(first):
-            return remote(part.at[pl.ds(first, 2), 1 - core], rd.at[pl.ds(first, 2)], d_s.at[first // 2], d_r.at[first // 2], partner)
-
-        def add_pair(first):
-            swap(first).wait()
-            for slot in (first, first + 1):
-                ssum[slot] = part[slot, core] + rd[slot]
-
-        def ring(slot, rows, dst, idx, dev):
-            return remote(ssum.at[slot, rows], dst, ring_s.at[idx], ring_r.at[idx], dev)
-
-        copies = [ring(0, lo, ra, 0, x_up), ring(0, hi, rb, 1, x_dn), ring(1, hi, fl.at[hi], 2, x_up), ring(2, lo, fr.at[lo], 3, x_dn),
-                  ring(1, lo, fl.at[lo], 4, x_up), ring(2, hi, fr.at[hi], 5, x_dn)]
-        with jax.named_scope("rstage"):
-            sigma(0, pl.ds(0, BOND))
-            swap(0).start()
-            sigma(2, pl.ds(0, 384))
-        with jax.named_scope("ring0"):
-            add_pair(0)
-            for cp in copies[:3]:
-                cp.start()
-        with jax.named_scope("rstage2"):
-            sigma(2, pl.ds(384, 256))
-            swap(2).start()
-        with jax.named_scope("xring"):
-            add_pair(2)
-            copies[3].start()
-            copies[0].wait_recv()
-            ssum[1, lo] = ssum[1, lo] + ra[...]
-            copies[4].start()
-            copies[1].wait_recv()
-            ssum[2, hi] = ssum[2, hi] + rb[...]
-            copies[5].start()
+        xo, xu, xd = wrap4(x + 2), wrap4(x + 1), wrap4(x - 1)
+
+        def sigma(cols):
+            for half in range(2):
+                res = lax.dot_general(rt[pl.ds(320 * half, 320), :], ys[cols, :], (((1,), (1,)), ((), ())), preferred_element_type=F32)
+                for idx in range(4):
+                    part[2 * half + idx // 2, idx % 2, :, cols] = res[idx * COLS:idx * COLS + COLS]
+
+        class Chunk:
+            def __init__(self, num, start, width):
+                cols = self.cols = pl.ds(start, width)
+                self.rows = start // LANES, (start + width) // LANES
+                self.swap = remote(part.at[:, 1 - core, :, cols], rd.at[:, :, cols], d_s.at[num], d_r.at[num], partner)
+                plan = ((xo, lo, ra, lo, x_up), (xo, hi, rb, lo, x_dn), (xu, hi, fl, hi, x_up), (xd, lo, fr, lo, x_dn), (xu, lo, fl, lo, x_up), (xd, hi, fr, hi, x_dn))
+                self.copies = [remote(ssum.at[chip, rows, cols], dst.at[to, cols], ring_s.at[6 * num + idx], ring_r.at[6 * num + idx], dev)
+                               for idx, (chip, rows, dst, to, dev) in enumerate(plan)]
+
+            def make_y(self):
+                lax.fori_loop(*self.rows, some_rows, 0)
+
+            def make(self):
+                sigma(self.cols)
+                self.swap.start()
+
+            def add(self):
+                self.swap.wait()
+                for chip in range(4):
+                    ssum[chip, :, self.cols] = part[chip, core, :, self.cols] + rd[chip, :, self.cols]
+                for cp in self.copies[:4]:
+                    cp.start()
+
+            def pass_on(self):
+                self.copies[0].wait_recv()
+                ssum[xu, lo, self.cols] = ssum[xu, lo, self.cols] + ra[:, self.cols]
+                self.copies[4].start()
+                self.copies[1].wait_recv()
+                ssum[xd, hi, self.cols] = ssum[xd, hi, self.cols] + rb[:, self.cols]
+                self.copies[5].start()
+
+            def finish(self):
+                for cp in self.copies[2:]:
+                    cp.wait_recv()
+                fin[pl.ds(0, COLS), self.cols] = ssum[x, :, self.cols] + fl[:, self.cols] + fr[:, self.cols]
+                for cp in self.copies:
+                    cp.wait_send()
+
+        one, two, three = (Chunk(*spec) for spec in ((0, 0, 256), (1, 256, 256), (2, 512, LANES)))
+        with jax.named_scope("w0"):
+            one.make_y()
+        with jax.named_scope("r0"):
+            one.make()
+        with jax.named_scope("w1"):
+            two.make_y()
+        with jax.named_scope("add0"):
+            one.add()
+        with jax.named_scope("r1"):
+            two.make()
+        with jax.named_scope("w2"):
+            three.make_y()
+        with jax.named_scope("add1"):
+            two.add()
+        with jax.named_scope("r2"):
+            three.make()
+        with jax.named_scope("pass0"):
+            one.pass_on()
+        with jax.named_scope("add2"):
+            three.add()
+        with jax.named_scope("pass1"):
+            two.pass_on()
+            three.pass_on()
+        with jax.named_scope("xfin"):
             v_cur = vt[cur]
             n_loc = total(v_cur * v_cur)
             c_loc = total(v_cur * vt[prev])
-            for cp in copies[2:]:
-                cp.wait_recv()
-            fin[pl.ds(0, COLS), :] = ssum[3] + fl[...] + fr[...]
-            for cp in copies:
-                cp.wait_send()
+            one.finish()
+            two.finish()
+            three.finish()
         with jax.named_scope("turn"):
             for b in range(5):
                 rows = pl.ds(LANES * b, LANES)
@@ -450,7 +456,11 @@
             w_val = t_val - ratio(s_loc, n_loc) * vt[cur]
             e_loc = total(w_val * w_val)
         with jax.named_scope("allred"):
-            n, s, e, c = all_reduce([n_loc, s_loc, e_loc, c_loc], out_start)
+            def last_start():
+                pl.when(step == NUM_STEPS - 1)(out_start)
+
+            n, s, e, c = all_reduce([n_loc, s_loc, e_loc, c_loc], last_start)
+            pl.when(step < NUM_STEPS - 1)(out_start)
         with jax.named_scope("vec2"):
             alpha = (s + beta * c) / VEC
             diff = alpha - ratio(s, n)
@@ -478,8 +488,8 @@
         vm((4, 4, 25, PAIR, LANES), BF16), vm((PAIR, 1280, LANES), BF16), vm((BOND, 4096), BF16), vm((4, 2) + block, F32),
         vm((4,) + block, F32), vm((4,) + block, F32), vm((ROWS, BOND), F32), vm((ROWS, BOND), F32), vm(block, F32), vm(block, F32),
         vm((LANES, BOND), F32), vm((BOND, LANES), F32), vm((3, BOND, LANES), F32), vm((8, COLS, LANES), F32), vm((8, COLS, LANES), F32), vm(block, F32),
-        vm((8, 1, LANES), F32), vm((PAIR, 1, LANES), F32),
-    ] + [dma((num,)) for num in (8, 8, 8, 8, 8, 8, 60, 60, 2, 2, 6, 6, 8, 8, PAIR, PAIR, 3)]
+        vm((LANES, 2, LANES), F32),
+    ] + [dma((num,)) for num in (8, 8, 8, 8, 8, 8, 60, 60, 3, 3, 18, 18)] + [dma, dma, dma((3,))]
     scal = jax.ShapeDtypeStruct((NUM_STEPS,), F32)
     return pl.pallas_call(
         kernel,

time: 310 us -> 295 us (0.952)
  Pallas kernels: 302 us -> 287 us
    pallas_call x1, Pallas kernels: 302 us -> 287 us  [run_kernel(): pl.pallas_call(kernel, out_shape=(jax.ShapeDtypeStruct((NUM_STEPS + 1,) +...]
where the time goes in v3:
time: 295 us; the launch traced here: 294 us
  Pallas kernels  287 us (97%)
  local copies, waits for them, and re-layouts  7 us (2%)
    pallas_call x1, Pallas kernels, run_kernel(): pl.pallas_call(kernel, out_shape=(jax.ShapeDtypeStruct((NUM_STEPS + 1,) +...  287 us

profile of v3, /device:TPU:1, one launch (start us, length us, event | category | flops | bytes accessed | tf_op | source)
XLA Modules:
  0.0 294.5 jit_solution(12571131894379665126)
XLA Ops:
  0.6 1.6 copy.7
  2.3 1.7 reshape.18.psi
  3.9 286.8 %lanczos.1 = (f32[7,80,640]{2,1,0:T(8,128)}, f32[6]{0:T(128)}, f32[6]{0:T(128)}) custom-call(f32[80,640]{1,0:T(8,128)} %reshape.18.psi, bf16[160,640]{1,0:T(8,128)(2,1)} %bitcast.5, bf16[512,16]{1,0:T(8,128)(2,1)} %bitcast.4, bf16[32,640,640]{2,1,0:T(8,128)(2,1)} %right.1), custom_call_target="tpu_custom_call" | custom-call | tf_op jit(solution)/shard_map/lanczos/pallas_call | solution.py:494
  290.8 0.0 copy-start.1
  290.8 0.0 copy-start
  290.8 2.7 reshape.21
  293.5 0.0 copy-done.1
  293.5 0.5 copy.10
  294.0 0.0 copy-done
  294.0 0.5 copy.11
Async XLA Ops:
  290.8 2.7 copy-start.1
  290.8 3.2 %copy-start = (f32[6]{0:T(128)S(1)}, f32[6]{0:T(128)}, u32[]{:S(2)}) copy-start(f32[6]{0:T(128)} %get-tuple-element.14) | copy-start | bytes 76

commit v4 on v3

--- a/solution.py
+++ b/solution.py
@@ -1,4 +1,4 @@
-import functools
+import itertools
 
 import jax
 import jax.numpy as jnp
@@ -16,10 +16,18 @@
 BOND, PAIR, TERMS = 640, 16, 32
 LANES = 128
 VEC = BOND * BOND * PAIR
+PARTS = ((((0, 2), (2, 5)), ((7, 2), (9, 6))), (((15, 1), (16, 4)), ((20, 1), (21, 4))))
+ORDER = "001000P1001010101Q10L1L1L1L1LLLL01"
+GSEM = 30
+FARTHEST = sorted(itertools.product(range(4), range(4), range(4), range(2)), key=lambda off: -sum(min(d, 4 - d) for d in off))[:-1]
 
 
 def remote(src, dst, send, recv, dev):
     return pltpu.make_async_remote_copy(src_ref=src, dst_ref=dst, send_sem=send, recv_sem=recv, device_id=(dev,), device_id_type=MESH)
+
+
+def tile_of(lane_tile, row_tile):
+    return 15 + 2 * lane_tile + row_tile - 2 if row_tile in (2, 3) else 3 * lane_tile + min(row_tile, 2)
 
 
 def lane_roll(val, shift):
@@ -83,6 +91,8 @@
     pl.semaphore_wait(barrier, LANES - 1)
 
     partner = me + 1 - 2 * core
+    places = ([wrap4(z + d) * 32 for d in range(4)], [wrap4(y + d) * 8 for d in range(4)], [wrap4(x + d) * 2 for d in range(4)], (core, 1 - core))
+    x_far = i * 8 + wrap4(x + 2) * 2 + core
     x_up, x_dn = i * 8 + wrap4(x + 1) * 2 + core, i * 8 + wrap4(x - 1) * 2 + core
     my_rows = rows_of(j)
 
@@ -107,12 +117,9 @@
         stat[me, pl.ds(0, 1), :] = row
         stat[me, pl.ds(1, 1), :] = jnp.broadcast_to(ratio(stats[1], stats[0]), (1, LANES))
 
-        def give(d, carry):
-            dev = lax.rem(me + d, LANES)
+        for off in FARTHEST:
+            dev = sum(spot[step] for spot, step in zip(places, off))
             remote(stat.at[me], stat.at[me], a_s, a_r, dev).start()
-            return carry
-
-        lax.fori_loop(1, LANES, give, 0, unroll=True)
         hook()
         most = stat.at[pl.ds(0, LANES - 1)]
         remote(most, most, a_s, a_r, partner).wait()
@@ -127,7 +134,7 @@
         ref = lall.at[src[0], src[1], rows]
         return remote(ref, ref, l_s.at[idx], l_r.at[idx], dev)
 
-    every, low, high = pl.ds(0, 160), pl.ds(0, COLS), pl.ds(COLS, COLS)
+    every = pl.ds(0, 160)
 
     def psi_sends():
         for jj in range(8):
@@ -139,6 +146,7 @@
         cp_l.wait()
         l_copy((x, core), every, 0, x_up).start()
         l_copy((x, core), every, 1, x_dn).start()
+        l_copy((x, core), every, 2, x_far).start()
         l_copy((x, core), every, 4, partner).start()
         spread = jnp.where(lax.broadcasted_iota(jnp.int32, (PAIR, 256), 1) // PAIR == lax.broadcasted_iota(jnp.int32, (PAIR, 256), 0), 1.0, 0.0).astype(BF16)
         same = lax.broadcasted_iota(jnp.int32, (256, 256), 1) % PAIR == lax.broadcasted_iota(jnp.int32, (256, 256), 0) // PAIR
@@ -162,17 +170,13 @@
     lower, upper, far = (wrap4(x - 1), core), (wrap4(x + 1), core), (wrap4(x + 2), core)
 
     def left_forward():
-        l_copy(lower, every, 0, x_up).wait_recv()
-        l_copy(lower, low, 2, x_up).start()
-        l_copy(upper, every, 1, x_dn).wait_recv()
-        l_copy(upper, high, 3, x_dn).start()
-        l_copy(lower, every, 5, partner).start()
-        l_copy(upper, every, 6, partner).start()
+        for idx, (block, way) in enumerate(((lower, x_up), (upper, x_dn), (far, x_far))):
+            l_copy(block, every, idx, way).wait_recv()
+            l_copy(block, every, 5 + idx, partner).start()
 
     def start_up():
         psi_sends()
         turn_right()
-        left_forward()
 
     psi_val = psi[...]
     zero = jnp.zeros((1, 1), F32)
@@ -190,13 +194,10 @@
     cp_v.start()
 
     def left_finish():
-        l_copy(far, low, 2, x_up).wait_recv()
-        l_copy(far, high, 3, x_dn).wait_recv()
-        l_copy(far, every, 7, partner).start()
         for idx, dx in ((4, 0), (5, 3), (6, 1), (7, 2)):
             l_copy((wrap4(x + dx), 1 - core), every, idx, partner).wait_recv()
-        for idx, rows in enumerate((every, every, low, high, every, every, every, every)):
-            l_copy((x, core), rows, idx, partner).wait_send()
+        for idx in (0, 1, 2, 4, 5, 6, 7):
+            l_copy((x, core), every, idx, partner).wait_send()
         for h in range(2):
             src = lax.broadcasted_iota(jnp.int32, (BOND, 768), 0)
             col = lax.broadcasted_iota(jnp.int32, (BOND, 768), 1)
@@ -268,6 +269,7 @@
         for b in range(4):
             for off, prt, idx in ((-1, 1, 7), (1, 0, 8), (2, 0, 10), (2, 1, 11)):
                 wait((offs[b], off), prt, 6 * b + idx)
+        yield
         for cp in done:
             cp.wait_send()
         yield
@@ -277,17 +279,21 @@
 
     y_ways, z_ways = (device(z, y + 1), device(z, y - 1), device(z, y + 2)), (device(z + 1, y), device(z - 1, y), device(z + 2, y))
 
-    def gather(busy):
-        def y_first(blk, prt):
-            return ug.at[wrap4(z + blk[1]), wrap4(y + blk[0]), pl.ds(*prt)]
-
-        def z_first(blk, prt):
-            return ug.at[wrap4(z + blk[0]), wrap4(y + blk[1]), pl.ds(*prt)]
-
-        both = [flow(0, y_ways, z_ways, y_first, ((0, 6), (6, 6))), flow(30, z_ways, y_ways, z_first, ((12, 6), (18, 7)))]
-        for idx, unused in enumerate(zip(*both)):
-            if idx in busy:
-                busy[idx]()
+    def y_first(blk, prt):
+        return ug.at[wrap4(z + blk[1]), wrap4(y + blk[0]), pl.ds(*prt)]
+
+    def z_first(blk, prt):
+        return ug.at[wrap4(z + blk[0]), wrap4(y + blk[1]), pl.ds(*prt)]
+
+    def gather(hooks):
+        flows = [[flow(GSEM * (2 * h + idx), *ways, ref, PARTS[h][idx]) for idx, (ways, ref) in enumerate((((y_ways, z_ways), y_first), ((z_ways, y_ways), z_first)))]
+                 for h in range(2)]
+        for mark in ORDER:
+            if mark in hooks:
+                hooks[mark]()
+            else:
+                for one in flows[int(mark)]:
+                    next(one)
 
     def out_copy(slot, jj, dev):
         return remote(sig.at[rows_of(jj)], out_recv.at[slot], out_s.at[jj], out_r.at[slot], dev)
@@ -321,39 +327,43 @@
                 half = [dense_tile(lambda idx, h=h: strided[8 * h + idx], lt) for h in range(2)]
                 for h in range(2):
                     for tt in range(2):
-                        ug[z, y, lt * 5 + 2 * h + tt] = half[h][PAIR * tt:PAIR * tt + PAIR].astype(BF16)
-                ug[z, y, lt * 5 + 4] = jnp.concatenate([half[0][32:ROWS], half[1][32:ROWS]], axis=0).astype(BF16)
-
-        def first_step():
-            @pl.when(step == 0)
-            def _():
-                left_finish()
-
-        def later_step():
+                        ug[z, y, tile_of(lt, 2 * h + tt)] = half[h][PAIR * tt:PAIR * tt + PAIR].astype(BF16)
+                ug[z, y, tile_of(lt, 4)] = jnp.concatenate([half[0][32:ROWS], half[1][32:ROWS]], axis=0).astype(BF16)
+
+        def early():
+            pl.when(step == 0)(left_forward)
+
+        def late():
+            pl.when(step == 0)(left_finish)
+
             @pl.when(step > 0)
             def _():
                 out_finish(step)
 
+        pieces = iter(range(8))
+
+        def left_piece():
+            pos = next(pieces)
+            h = pos // 4
+            cols = []
+            for r in (2 * pos, 2 * pos + 1):
+                rows = [take_piece(lambda t, tr=tr: ug[:, :, tile_of(t, tr)].reshape(256, LANES), r % 8) for tr in (2 * h, 2 * h + 1, 4)]
+                cols.append(jnp.concatenate(rows, axis=0))
+            rhs = jnp.concatenate(cols, axis=1)
+            for mc in range(2):
+                rows = pl.ds(BOND * mc, BOND)
+                res = jnp.dot(lh[h, rows, :], rhs, preferred_element_type=F32).astype(BF16)
+                for rr in range(2):
+                    xs[2 * pos + rr, rows, :] = res[:, LANES * rr:LANES * rr + LANES]
+
+        def named(name, call):
+            def run():
+                with jax.named_scope(name):
+                    call()
+            return run
+
         with jax.named_scope("gather"):
-            gather({1: first_step, 6: later_step})
-
-        def left_half(h, carry):
-            for rp in range(4):
-                cols = []
-                for rr in range(2):
-                    idx = 2 * rp + rr
-                    rows = [take_piece(lambda t, tr=tr: ug[:, :, t * 5 + tr].reshape(256, LANES), idx) for tr in (2 * h, 2 * h + 1, 4)]
-                    cols.append(jnp.concatenate(rows, axis=0))
-                rhs = jnp.concatenate(cols, axis=1)
-                for mc in range(2):
-                    rows = pl.ds(BOND * mc, BOND)
-                    res = jnp.dot(lh[h, rows, :], rhs, preferred_element_type=F32).astype(BF16)
-                    for rr in range(2):
-                        xs[h * 8 + 2 * rp + rr, rows, :] = res[:, LANES * rr:LANES * rr + LANES]
-            return carry
-
-        with jax.named_scope("lstage"):
-            lax.fori_loop(0, 2, left_half, 0)
+            gather({"P": early, "Q": named("late", late), "L": named("left", left_piece)})
 
         def some_rows(ap, carry):
             for pr in range(4):
@@ -489,7 +499,7 @@
         vm((4,) + block, F32), vm((4,) + block, F32), vm((ROWS, BOND), F32), vm((ROWS, BOND), F32), vm(block, F32), vm(block, F32),
         vm((LANES, BOND), F32), vm((BOND, LANES), F32), vm((3, BOND, LANES), F32), vm((8, COLS, LANES), F32), vm((8, COLS, LANES), F32), vm(block, F32),
         vm((LANES, 2, LANES), F32),
-    ] + [dma((num,)) for num in (8, 8, 8, 8, 8, 8, 60, 60, 3, 3, 18, 18)] + [dma, dma, dma((3,))]
+    ] + [dma((num,)) for num in (8, 8, 8, 8, 8, 8, 4 * GSEM, 4 * GSEM, 3, 3, 18, 18)] + [dma, dma, dma((3,))]
     scal = jax.ShapeDtypeStruct((NUM_STEPS,), F32)
     return pl.pallas_call(
         kernel,

time: 295 us -> 302 us (1.024)
  Pallas kernels: 287 us -> 294 us
    pallas_call x1, Pallas kernels: 287 us -> 294 us  [run_kernel(): pl.pallas_call(kernel, out_shape=(jax.ShapeDtypeStruct((NUM_STEPS + 1,) +...]
where the time goes in v4:
time: 302 us
  Pallas kernels  294 us (97%)
  local copies, waits for them, and re-layouts  7 us (2%)
    pallas_call x1, Pallas kernels, run_kernel(): pl.pallas_call(kernel, out_shape=(jax.ShapeDtypeStruct((NUM_STEPS + 1,) +...  294 us

profile of v4, /device:TPU:1, one launch (start us, length us, event | category | flops | bytes accessed | tf_op | source)
XLA Modules:
  0.0 301.7 jit_solution(12756219308383161285)
XLA Ops:
  0.6 1.6 copy.7
  2.3 1.7 reshape.18.psi
  3.9 294.1 %lanczos.1 = (f32[7,80,640]{2,1,0:T(8,128)}, f32[6]{0:T(128)}, f32[6]{0:T(128)}) custom-call(f32[80,640]{1,0:T(8,128)} %reshape.18.psi, bf16[160,640]{1,0:T(8,128)(2,1)} %bitcast.5, bf16[512,16]{1,0:T(8,128)(2,1)} %bitcast.4, bf16[32,640,640]{2,1,0:T(8,128)(2,1)} %right.1), custom_call_target="tpu_custom_call" | custom-call | tf_op jit(solution)/shard_map/lanczos/pallas_call | solution.py:504
  298.0 0.0 copy-start.1
  298.0 0.0 copy-start
  298.1 2.7 reshape.21
  300.7 0.0 copy-done.1
  300.7 0.5 copy.10
  301.2 0.0 copy-done
  301.2 0.5 copy.11
Async XLA Ops:
  298.0 2.7 copy-start.1
  298.0 3.2 %copy-start = (f32[6]{0:T(128)S(1)}, f32[6]{0:T(128)}, u32[]{:S(2)}) copy-start(f32[6]{0:T(128)} %get-tuple-element.14) | copy-start | bytes 76

commit v5 on v4

--- a/solution.py
+++ b/solution.py
@@ -2,6 +2,7 @@
 
 import jax
 import jax.numpy as jnp
+import numpy as np
 from jax import lax
 from jax.experimental import pallas as pl
 from jax.experimental.pallas import tpu as pltpu
@@ -16,10 +17,18 @@
 BOND, PAIR, TERMS = 640, 16, 32
 LANES = 128
 VEC = BOND * BOND * PAIR
-PARTS = ((((0, 2), (2, 5)), ((7, 2), (9, 6))), (((15, 1), (16, 4)), ((20, 1), (21, 4))))
-ORDER = "001000P1001010101Q10L1L1L1L1LLLL01"
+PARTS = ((((0, 4), (4, 3)), ((7, 4), (11, 4))), (((15, 2), (17, 3)), ((20, 3), (23, 2))))
+ORDER = "001000P1111001Q10011010L1L01"
 GSEM = 30
 FARTHEST = sorted(itertools.product(range(4), range(4), range(4), range(2)), key=lambda off: -sum(min(d, 4 - d) for d in off))[:-1]
+
+
+def left_order():
+    col = np.arange(1024)
+    group, tail = (col % 256) // PAIR, col >= 512
+    src = np.where(tail, ROWS * group + 32 + col % 8, ROWS * group + PAIR * (col // 256) + col % PAIR)
+    used = ~tail | ((col // 8) % 2 == (col >= 768))
+    return jnp.asarray((np.arange(BOND)[:, None] == src) & used, BF16)
 
 
 def remote(src, dst, send, recv, dev):
@@ -59,7 +68,7 @@
     return out
 
 
-def kernel(psi, left, pair, right, vecs, alphas, betas, lall, lh, wbig, rtmp, rt, ug, xs, ys, part, rd, ssum, ra, rb, fl, fr, fin,
+def kernel(psi, left, pair, order, right, vecs, alphas, betas, lall, lh, wbig, rtmp, rt, ug, xs, ys, part, rd, ssum, ra, rb, fl, fr, fin,
            sig, vt, piece_buf, out_recv, outv, stat, psi_s, psi_r, l_s, l_r, out_s, out_r, g_s, g_r, d_s, d_r,
            ring_s, ring_r, a_s, a_r, loc):
     me = lax.axis_index("rows")
@@ -122,7 +131,8 @@
             remote(stat.at[me], stat.at[me], a_s, a_r, dev).start()
         hook()
         most = stat.at[pl.ds(0, LANES - 1)]
-        remote(most, most, a_s, a_r, partner).wait()
+        with jax.named_scope("arwait"):
+            remote(most, most, a_s, a_r, partner).wait()
         rows = stat[:, pl.ds(0, 1), :]
         sums = jnp.sum(rows, axis=0)
         n, s, e, c = (jnp.sum(jnp.where(row_lane == idx, sums, 0.0), axis=1, keepdims=True) for idx in range(4))
@@ -175,8 +185,10 @@
             l_copy(block, every, 5 + idx, partner).start()
 
     def start_up():
-        psi_sends()
-        turn_right()
+        with jax.named_scope("psi"):
+            psi_sends()
+        with jax.named_scope("turnr"):
+            turn_right()
 
     psi_val = psi[...]
     zero = jnp.zeros((1, 1), F32)
@@ -198,20 +210,14 @@
             l_copy((wrap4(x + dx), 1 - core), every, idx, partner).wait_recv()
         for idx in (0, 1, 2, 4, 5, 6, 7):
             l_copy((x, core), every, idx, partner).wait_send()
-        for h in range(2):
-            src = lax.broadcasted_iota(jnp.int32, (BOND, 768), 0)
-            col = lax.broadcasted_iota(jnp.int32, (BOND, 768), 1)
-            group = (col % 256) // PAIR
-            main = ROWS * group + PAIR * (col // 256) + col % PAIR
-            tail = jnp.where((col // 8) % 2 == h, ROWS * group + 32 + col % 8, -1)
-            order = jnp.where(src == jnp.where(col < 512, main, tail), 1.0, 0.0).astype(BF16)
-
-            def body(t, carry):
-                rows = pl.ds(pl.multiple_of(t * 160, 160), 160)
-                lh[h, rows, :] = jnp.dot(lall[t // 2, t % 2], order, preferred_element_type=F32).astype(BF16)
-                return carry
-
-            lax.fori_loop(0, 8, body, 0)
+        def body(t, carry):
+            rows = pl.ds(pl.multiple_of(t * 160, 160), 160)
+            res = jnp.dot(lall[t // 2, t % 2], order[...], preferred_element_type=F32).astype(BF16)
+            for h in range(2):
+                lh[h, rows, :] = jnp.concatenate([res[:, :512], res[:, 512 + 256 * h:768 + 256 * h]], axis=1)
+            return carry
+
+        lax.fori_loop(0, 8, body, 0)
 
     def flow(base, firsts, seconds, ref, parts):
         done = []
@@ -340,21 +346,21 @@
             def _():
                 out_finish(step)
 
-        pieces = iter(range(8))
-
-        def left_piece():
-            pos = next(pieces)
-            h = pos // 4
-            cols = []
-            for r in (2 * pos, 2 * pos + 1):
-                rows = [take_piece(lambda t, tr=tr: ug[:, :, tile_of(t, tr)].reshape(256, LANES), r % 8) for tr in (2 * h, 2 * h + 1, 4)]
-                cols.append(jnp.concatenate(rows, axis=0))
-            rhs = jnp.concatenate(cols, axis=1)
-            for mc in range(2):
-                rows = pl.ds(BOND * mc, BOND)
-                res = jnp.dot(lh[h, rows, :], rhs, preferred_element_type=F32).astype(BF16)
-                for rr in range(2):
-                    xs[2 * pos + rr, rows, :] = res[:, LANES * rr:LANES * rr + LANES]
+        halves = iter(range(2))
+
+        def left_half():
+            h = next(halves)
+            for pos in range(4 * h, 4 * h + 4):
+                cols = []
+                for r in (2 * pos, 2 * pos + 1):
+                    rows = [take_piece(lambda t, tr=tr: ug[:, :, tile_of(t, tr)].reshape(256, LANES), r % 8) for tr in (2 * h, 2 * h + 1, 4)]
+                    cols.append(jnp.concatenate(rows, axis=0))
+                rhs = jnp.concatenate(cols, axis=1)
+                for mc in range(2):
+                    rows = pl.ds(BOND * mc, BOND)
+                    res = jnp.dot(lh[h, rows, :], rhs, preferred_element_type=F32).astype(BF16)
+                    for rr in range(2):
+                        xs[2 * pos + rr, rows, :] = res[:, LANES * rr:LANES * rr + LANES]
 
         def named(name, call):
             def run():
@@ -363,7 +369,7 @@
             return run
 
         with jax.named_scope("gather"):
-            gather({"P": early, "Q": named("late", late), "L": named("left", left_piece)})
+            gather({"P": early, "Q": named("late", late), "L": named("left", left_half)})
 
         def some_rows(ap, carry):
             for pr in range(4):
@@ -488,7 +494,7 @@
     cp_v.wait()
 
 
-def run_kernel(psi, left, pair, right):
+def run_kernel(psi, left, pair, order, right):
     vmem, anys, smem = (pl.BlockSpec(memory_space=space) for space in (pltpu.VMEM, pl.ANY, pltpu.SMEM))
     dma = pltpu.SemaphoreType.DMA
     vm = pltpu.VMEM
@@ -504,19 +510,19 @@
     return pl.pallas_call(
         kernel,
         out_shape=(jax.ShapeDtypeStruct((NUM_STEPS + 1,) + block, F32), scal, scal),
-        in_specs=[vmem, anys, vmem, anys],
+        in_specs=[vmem, anys, vmem, vmem, anys],
         out_specs=(anys, smem, smem),
         scratch_shapes=scratch,
         compiler_params=pltpu.CompilerParams(collective_id=0, has_side_effects=True, vmem_limit_bytes=67043328),
         name="lanczos",
-    )(psi, left, pair, right)
+    )(psi, left, pair, order, right)
 
 
 def solution(mesh):
     def local_run(wave_rows, left_rows, op_pair, right_env):
         psi = wave_rows.reshape(COLS, BOND)
         left = jnp.transpose(left_rows, (1, 0, 2)).reshape(160, BOND)
-        vecs, alphas, betas = run_kernel(psi, left, op_pair.reshape(512, PAIR), right_env)
+        vecs, alphas, betas = run_kernel(psi, left, op_pair.reshape(512, PAIR), left_order(), right_env)
         return vecs.reshape(7, 5, 4, 4, BOND), alphas, betas
 
     rows = "rows"

time: 302 us -> 286 us (0.947)
  Pallas kernels: 294 us -> 278 us
    pallas_call x1, Pallas kernels: 294 us -> 278 us  [run_kernel(): pl.pallas_call(kernel, out_shape=(jax.ShapeDtypeStruct((NUM_STEPS + 1,) +...]
where the time goes in v5:
time: 286 us; the launch traced here: 285 us
  Pallas kernels  278 us (97%)
  local copies, waits for them, and re-layouts  7 us (2%)
    pallas_call x1, Pallas kernels, run_kernel(): pl.pallas_call(kernel, out_shape=(jax.ShapeDtypeStruct((NUM_STEPS + 1,) +...  278 us

profile of v5, /device:TPU:1, one launch (start us, length us, event | category | flops | bytes accessed | tf_op | source)
XLA Modules:
  0.0 285.3 jit_solution(18314103219082381996)
XLA Ops:
  0.6 1.6 copy.8
  2.3 1.7 reshape.18.psi
  3.9 277.7 %lanczos.1 = (f32[7,80,640]{2,1,0:T(8,128)}, f32[6]{0:T(128)}, f32[6]{0:T(128)}) custom-call(f32[80,640]{1,0:T(8,128)} %reshape.18.psi, bf16[160,640]{1,0:T(8,128)(2,1)} %bitcast.5, bf16[512,16]{1,0:T(8,128)(2,1)} %bitcast.4, bf16[640,1024]{1,0:T(8,128)(2,1)} %constant.2.clone.order, bf16[32,640,640]{2,1,0:T(8,128)(2,1)} %right.1), custom_call_target="tpu_custom_call" | custom-call | tf_op jit(solution)/shard_map/lanczos/pallas_call | solution.py:510
  281.6 0.0 copy-start.1
  281.6 0.0 copy-start
  281.6 2.7 reshape.21
  284.3 0.0 copy-done.1
  284.3 0.5 copy.11
  284.8 0.0 copy-done
  284.8 0.5 copy.12
Async XLA Ops:
  281.6 2.7 copy-start.1
  281.6 3.2 %copy-start = (f32[6]{0:T(128)S(1)}, f32[6]{0:T(128)}, u32[]{:S(2)}) copy-start(f32[6]{0:T(128)} %get-tuple-element.14) | copy-start | bytes 76

commit v6 on v5

--- a/solution.py
+++ b/solution.py
@@ -16,6 +16,7 @@
 ROWS, COLS = 40, 80
 BOND, PAIR, TERMS = 640, 16, 32
 LANES = 128
+GC, RING, WIDE = 8, 4, 256
 VEC = BOND * BOND * PAIR
 PARTS = ((((0, 4), (4, 3)), ((7, 4), (11, 4))), (((15, 2), (17, 3)), ((20, 3), (23, 2))))
 ORDER = "001000P1111001Q10011010L1L01"
@@ -25,9 +26,9 @@
 
 def left_order():
     col = np.arange(1024)
-    group, tail = (col % 256) // PAIR, col >= 512
-    src = np.where(tail, ROWS * group + 32 + col % 8, ROWS * group + PAIR * (col // 256) + col % PAIR)
-    used = ~tail | ((col // 8) % 2 == (col >= 768))
+    group, tail = (col % WIDE) // PAIR, col >= 512
+    src = np.where(tail, ROWS * group + 32 + col % GC, ROWS * group + PAIR * (col // WIDE) + col % PAIR)
+    used = ~tail | ((col // GC) % 2 == (col >= 768))
     return jnp.asarray((np.arange(BOND)[:, None] == src) & used, BF16)
 
 
@@ -57,9 +58,22 @@
     return jnp.where(lane < COLS, out, jnp.zeros_like(out))
 
 
+def merge_three(one, two, three=None):
+    if three is None:
+        return one, two
+    inner = lane_iota(one) < COLS
+    return jnp.where(inner, one, lane_roll(three, COLS)), jnp.where(inner, two, lane_roll(three, COLS - 48))
+
+
+def split_three(left, right):
+    lane, zero = lane_iota(left), jnp.zeros_like(left)
+    three = jnp.where(lane < 48, lane_roll(left, -COLS), jnp.where(lane < COLS, lane_roll(right, 48 - COLS), zero))
+    return jnp.where(lane < COLS, left, zero), jnp.where(lane < COLS, right, zero), three
+
+
 def dense_tile(pieces, tile):
     out = None
-    for idx in range(8):
+    for idx in range(GC):
         shift = COLS * idx - LANES * tile
         if shift <= -COLS or shift >= LANES:
             continue
@@ -70,43 +84,59 @@
 
 def kernel(psi, left, pair, order, right, vecs, alphas, betas, lall, lh, wbig, rtmp, rt, ug, xs, ys, part, rd, ssum, ra, rb, fl, fr, fin,
            sig, vt, piece_buf, out_recv, outv, stat, psi_s, psi_r, l_s, l_r, out_s, out_r, g_s, g_r, d_s, d_r,
-           ring_s, ring_r, a_s, a_r, loc):
+           ring_s, ring_r, a_s, a_r, loc, ready):
     me = lax.axis_index("rows")
     core = lax.rem(me, 2)
-    x = lax.rem(me // 2, 4)
-    y = lax.rem(me // 8, 4)
+    x = lax.rem(me // 2, RING)
+    y = lax.rem(me // GC, RING)
     z = me // 32
-    i = me // 8
-    j = lax.rem(me, 8)
+    i = me // GC
+    t_me = lax.rem(me, GC)
+    label = lax.rem(me + x + y + z, 2)
+    j = x * 2 + label
     lo, hi = pl.ds(0, ROWS), pl.ds(ROWS, ROWS)
 
     def wrap4(val):
-        return lax.rem(val + 4, 4)
-
-    def in_row(dj):
-        jj = lax.rem(j + dj, 8)
-        return jj, i * 8 + jj
+        return lax.rem(val + RING, RING)
+
+    def in_row(d):
+        tt = lax.rem(t_me + d, GC)
+        return tt, tt - lax.rem(tt, 2) + lax.rem(tt + tt // 2 + y + z, 2), i * GC + tt
 
     def rows_of(jj):
         return pl.ds(pl.multiple_of(jj * COLS, COLS), COLS)
 
     barrier = pltpu.get_barrier_semaphore()
 
-    def greet(d, carry):
-        pl.semaphore_signal(barrier, inc=1, device_id=(lax.rem(me + d, LANES),), device_id_type=MESH)
-        return carry
-
-    lax.fori_loop(1, LANES, greet, 0)
-    pl.semaphore_wait(barrier, LANES - 1)
+    def col_dev(di):
+        ii = lax.rem(i + di, PAIR)
+        return ii * GC + x * 2 + lax.rem(label + x + ii + ii // RING, 2)
+
+    for d in range(1, GC):
+        pl.semaphore_signal(barrier, inc=1, device_id=(in_row(d)[2],), device_id_type=MESH)
+    for di in range(1, PAIR):
+        pl.semaphore_signal(barrier, inc=1, device_id=(col_dev(di),), device_id_type=MESH)
+    pl.semaphore_wait(barrier, 22)
+    for di in range(1, PAIR):
+        pl.semaphore_signal(ready, inc=1, device_id=(col_dev(di),), device_id_type=MESH)
 
     partner = me + 1 - 2 * core
-    places = ([wrap4(z + d) * 32 for d in range(4)], [wrap4(y + d) * 8 for d in range(4)], [wrap4(x + d) * 2 for d in range(4)], (core, 1 - core))
-    x_far = i * 8 + wrap4(x + 2) * 2 + core
-    x_up, x_dn = i * 8 + wrap4(x + 1) * 2 + core, i * 8 + wrap4(x - 1) * 2 + core
-    my_rows = rows_of(j)
-
-    cp_r = pltpu.make_async_copy(right.at[:, my_rows, :], rtmp.at[:, pl.ds(0, COLS), :], loc.at[0])
-    cp_r.start()
+    places = ([wrap4(z + d) * 32 for d in range(RING)], [wrap4(y + d) * GC for d in range(RING)], [wrap4(x + d) * 2 for d in range(RING)], (core, 1 - core))
+    x_up, x_dn = i * GC + wrap4(x + 1) * 2 + 1 - core, i * GC + wrap4(x - 1) * 2 + 1 - core
+    left_up, left_dn, left_far = (i * GC + wrap4(x + d) * 2 + core for d in (1, -1, 2))
+    my_rows = rows_of(t_me)
+
+    def fetch_right(first, last, row, width):
+        def body(m, carry):
+            src = right.at[3 * m + first, pl.ds(pl.multiple_of(j * COLS + row, PAIR), width), :]
+            pltpu.make_async_copy(src, rtmp.at[pl.ds(pl.multiple_of(WIDE * m + last, PAIR), width), :], loc.at[0]).start()
+            return carry
+        return body
+
+    lax.fori_loop(0, 11, fetch_right(0, 0, 0, COLS), 0)
+    lax.fori_loop(0, 11, fetch_right(1, LANES, 0, COLS), 0)
+    lax.fori_loop(0, 10, fetch_right(2, COLS, 0, 48), 0)
+    lax.fori_loop(0, 10, fetch_right(2, LANES + COLS, 48, 32), 0)
     cp_l = pltpu.make_async_copy(left, lall.at[x, core], loc.at[1])
     cp_l.start()
 
@@ -135,7 +165,7 @@
             remote(most, most, a_s, a_r, partner).wait()
         rows = stat[:, pl.ds(0, 1), :]
         sums = jnp.sum(rows, axis=0)
-        n, s, e, c = (jnp.sum(jnp.where(row_lane == idx, sums, 0.0), axis=1, keepdims=True) for idx in range(4))
+        n, s, e, c = (jnp.sum(jnp.where(row_lane == idx, sums, 0.0), axis=1, keepdims=True) for idx in range(RING))
         diff = stat[:, pl.ds(1, 1), :] - ratio(s, n)[None]
         moved = jnp.sum(diff * rows * diff, axis=0)
         return n, s, e + jnp.sum(jnp.where(row_lane == 0, moved, 0.0), axis=1, keepdims=True), c
@@ -146,41 +176,48 @@
 
     every = pl.ds(0, 160)
 
-    def psi_sends():
-        for jj in range(8):
+    def psi_pieces():
+        for jj in range(GC):
             piece_buf[jj] = take_piece(lambda t: psi[:, LANES * t:LANES * t + LANES], jj)
         vt[0, my_rows, :] = piece_buf[j]
-        for dj in range(1, 8):
-            jj, dev = in_row(dj)
-            remote(piece_buf.at[jj], vt.at[0, my_rows], psi_s.at[jj], psi_r.at[j], dev).start()
-        cp_l.wait()
-        l_copy((x, core), every, 0, x_up).start()
-        l_copy((x, core), every, 1, x_dn).start()
-        l_copy((x, core), every, 2, x_far).start()
-        l_copy((x, core), every, 4, partner).start()
-        spread = jnp.where(lax.broadcasted_iota(jnp.int32, (PAIR, 256), 1) // PAIR == lax.broadcasted_iota(jnp.int32, (PAIR, 256), 0), 1.0, 0.0).astype(BF16)
-        same = lax.broadcasted_iota(jnp.int32, (256, 256), 1) % PAIR == lax.broadcasted_iota(jnp.int32, (256, 256), 0) // PAIR
+        spread = jnp.where(lax.broadcasted_iota(jnp.int32, (PAIR, WIDE), 1) // PAIR == lax.broadcasted_iota(jnp.int32, (PAIR, WIDE), 0), 1.0, 0.0).astype(BF16)
+        same = lax.broadcasted_iota(jnp.int32, (WIDE, WIDE), 1) % PAIR == lax.broadcasted_iota(jnp.int32, (WIDE, WIDE), 0) // PAIR
         for h in range(2):
-            wide = jnp.dot(pair[pl.ds(256 * h, 256), :], spread, preferred_element_type=F32)
+            wide = jnp.dot(pair[pl.ds(WIDE * h, WIDE), :], spread, preferred_element_type=F32)
             wbig[h] = jnp.where(same, wide, 0.0).astype(BF16)
         vt[2] = jnp.zeros((BOND, LANES), F32)
         fin[...] = jnp.zeros((LANES, BOND), F32)
 
+    def psi_sends():
+        for d in range(1, GC):
+            tt, jj, dev = in_row(d)
+            remote(piece_buf.at[jj], vt.at[0, my_rows], psi_s.at[tt], psi_r.at[t_me], dev).start()
+        cp_l.wait()
+        l_copy((x, core), every, 0, left_up).start()
+        l_copy((x, core), every, 1, left_dn).start()
+        l_copy((x, core), every, 2, left_far).start()
+        l_copy((x, core), every, RING, partner).start()
+
     def turn_right():
-        cp_r.wait()
+        some = rtmp.at[pl.ds(0, TERMS * COLS), :]
+        pltpu.make_async_copy(some, some, loc.at[0]).wait()
+        for m in range(11):
+            rtmp[pl.ds(WIDE * m + 240, PAIR), :] = jnp.zeros((PAIR, BOND), BF16)
+        for start in (COLS, LANES + COLS):
+            rtmp[pl.ds(2560 + start, 48), :] = jnp.zeros((48, BOND), BF16)
 
         def body(k, carry):
-            rtmp[k, pl.ds(COLS, 48), :] = jnp.zeros((48, BOND), BF16)
+            cols = pl.ds(pl.multiple_of(k * LANES, LANES), LANES)
             for b in range(5):
-                rt[pl.ds(LANES * b, LANES), pl.ds(pl.multiple_of(k * LANES, LANES), LANES)] = rtmp[k, :, pl.ds(LANES * b, LANES)].T
+                rt[pl.ds(LANES * b, LANES), cols] = rtmp[cols, pl.ds(LANES * b, LANES)].T
             return carry
 
-        lax.fori_loop(0, TERMS, body, 0)
+        lax.fori_loop(0, 22, body, 0)
 
     lower, upper, far = (wrap4(x - 1), core), (wrap4(x + 1), core), (wrap4(x + 2), core)
 
     def left_forward():
-        for idx, (block, way) in enumerate(((lower, x_up), (upper, x_dn), (far, x_far))):
+        for idx, (block, way) in enumerate(((lower, left_up), (upper, left_dn), (far, left_far))):
             l_copy(block, every, idx, way).wait_recv()
             l_copy(block, every, 5 + idx, partner).start()
 
@@ -190,14 +227,16 @@
         with jax.named_scope("turnr"):
             turn_right()
 
+    psi_pieces()
     psi_val = psi[...]
+    pl.semaphore_wait(ready, PAIR - 1)
     zero = jnp.zeros((1, 1), F32)
     n_psi = all_reduce([total(psi_val * psi_val), zero], start_up)[0]
     inv_norm = 1.0 / jnp.sqrt(n_psi / VEC)
 
-    for dj in range(1, 8):
-        jj, dev = in_row(dj)
-        cp = remote(piece_buf.at[jj], vt.at[0, rows_of(jj)], psi_s.at[jj], psi_r.at[jj], dev)
+    for d in range(1, GC):
+        tt, jj, dev = in_row(d)
+        cp = remote(piece_buf.at[jj], vt.at[0, rows_of(tt)], psi_s.at[tt], psi_r.at[tt], dev)
         cp.wait_recv()
         cp.wait_send()
     vt[0] = vt[0] * inv_norm
@@ -206,18 +245,18 @@
     cp_v.start()
 
     def left_finish():
-        for idx, dx in ((4, 0), (5, 3), (6, 1), (7, 2)):
+        for idx, dx in ((RING, 0), (5, 3), (6, 1), (7, 2)):
             l_copy((wrap4(x + dx), 1 - core), every, idx, partner).wait_recv()
-        for idx in (0, 1, 2, 4, 5, 6, 7):
+        for idx in (0, 1, 2, RING, 5, 6, 7):
             l_copy((x, core), every, idx, partner).wait_send()
         def body(t, carry):
             rows = pl.ds(pl.multiple_of(t * 160, 160), 160)
             res = jnp.dot(lall[t // 2, t % 2], order[...], preferred_element_type=F32).astype(BF16)
             for h in range(2):
-                lh[h, rows, :] = jnp.concatenate([res[:, :512], res[:, 512 + 256 * h:768 + 256 * h]], axis=1)
+                lh[h, rows, :] = jnp.concatenate([res[:, :512], res[:, 512 + WIDE * h:768 + WIDE * h]], axis=1)
             return carry
 
-        lax.fori_loop(0, 8, body, 0)
+        lax.fori_loop(0, GC, body, 0)
 
     def flow(base, firsts, seconds, ref, parts):
         done = []
@@ -246,7 +285,7 @@
         for prt, way in ((0, 0), (1, 1), (1, 0), (0, 1)):
             send((0, 0), prt, 2 * way + prt, firsts[way])
         for prt in range(2):
-            send((0, 0), prt, 4 + prt, firsts[2])
+            send((0, 0), prt, RING + prt, firsts[2])
         yield
         second(0, 0)
         second(0, 1)
@@ -264,26 +303,26 @@
         yield
         second_forward(0)
         yield
-        wait((2, 0), 0, 4)
+        wait((2, 0), 0, RING)
         second(3, 0)
         wait((2, 0), 1, 5)
         second(3, 1)
         yield
-        for b in range(1, 4):
+        for b in range(1, RING):
             second_forward(b)
             yield
-        for b in range(4):
-            for off, prt, idx in ((-1, 1, 7), (1, 0, 8), (2, 0, 10), (2, 1, 11)):
+        for b in range(RING):
+            for off, prt, idx in ((-1, 1, 7), (1, 0, GC), (2, 0, 10), (2, 1, 11)):
                 wait((offs[b], off), prt, 6 * b + idx)
         yield
         for cp in done:
             cp.wait_send()
         yield
 
-    def device(zz, yy):
-        return (wrap4(zz) * 4 + wrap4(yy)) * 8 + j
-
-    y_ways, z_ways = (device(z, y + 1), device(z, y - 1), device(z, y + 2)), (device(z + 1, y), device(z - 1, y), device(z + 2, y))
+    def device(dz, dy):
+        return (wrap4(z + dz) * RING + wrap4(y + dy)) * GC + x * 2 + (1 - core if (dz + dy) % 2 else core)
+
+    y_ways, z_ways = [device(0, d) for d in (1, -1, 2)], [device(d, 0) for d in (1, -1, 2)]
 
     def y_first(blk, prt):
         return ug.at[wrap4(z + blk[1]), wrap4(y + blk[0]), pl.ds(*prt)]
@@ -301,22 +340,22 @@
                 for one in flows[int(mark)]:
                     next(one)
 
-    def out_copy(slot, jj, dev):
-        return remote(sig.at[rows_of(jj)], out_recv.at[slot], out_s.at[jj], out_r.at[slot], dev)
+    def out_copy(slot, tt, dev):
+        return remote(sig.at[rows_of(tt)], out_recv.at[slot], out_s.at[tt], out_r.at[slot], dev)
 
     def out_start():
-        for dj in range(1, 8):
-            jj, dev = in_row(dj)
-            out_copy(j, jj, dev).start()
+        for d in range(1, GC):
+            tt, jj, dev = in_row(d)
+            out_copy(j, tt, dev).start()
         out_recv[j] = sig[my_rows, :]
 
     def out_finish(step):
-        for dj in range(1, 8):
-            jj, dev = in_row(dj)
-            out_copy(jj, jj, dev).wait_recv()
-            out_copy(j, jj, dev).wait_send()
+        for d in range(1, GC):
+            tt, jj, dev = in_row(d)
+            out_copy(jj, tt, dev).wait_recv()
+            out_copy(j, tt, dev).wait_send()
         cp_v.wait()
-        alpha, inv = fin[pl.ds(COLS, 1), pl.ds(0, 1)], fin[pl.ds(COLS + 8, 1), pl.ds(0, 1)]
+        alpha, inv = fin[pl.ds(COLS, 1), pl.ds(0, 1)], fin[pl.ds(COLS + GC, 1), pl.ds(0, 1)]
         for tile in range(5):
             lanes = pl.ds(LANES * tile, LANES)
             outv[:, lanes] = (dense_tile(lambda idx: out_recv[idx], tile) - alpha * outv[:, lanes]) * inv
@@ -330,11 +369,11 @@
         with jax.named_scope("pack"):
             strided = [vt[cur, pl.ds(r, ROWS, stride=PAIR), :] for r in range(PAIR)]
             for lt in range(5):
-                half = [dense_tile(lambda idx, h=h: strided[8 * h + idx], lt) for h in range(2)]
+                half = [dense_tile(lambda idx, h=h: strided[GC * h + idx], lt) for h in range(2)]
                 for h in range(2):
                     for tt in range(2):
                         ug[z, y, tile_of(lt, 2 * h + tt)] = half[h][PAIR * tt:PAIR * tt + PAIR].astype(BF16)
-                ug[z, y, tile_of(lt, 4)] = jnp.concatenate([half[0][32:ROWS], half[1][32:ROWS]], axis=0).astype(BF16)
+                ug[z, y, tile_of(lt, RING)] = jnp.concatenate([half[0][32:ROWS], half[1][32:ROWS]], axis=0).astype(BF16)
 
         def early():
             pl.when(step == 0)(left_forward)
@@ -350,17 +389,18 @@
 
         def left_half():
             h = next(halves)
-            for pos in range(4 * h, 4 * h + 4):
-                cols = []
-                for r in (2 * pos, 2 * pos + 1):
-                    rows = [take_piece(lambda t, tr=tr: ug[:, :, tile_of(t, tr)].reshape(256, LANES), r % 8) for tr in (2 * h, 2 * h + 1, 4)]
-                    cols.append(jnp.concatenate(rows, axis=0))
-                rhs = jnp.concatenate(cols, axis=1)
+            for group in range(3):
+                first = 3 * group
+                got = []
+                for r in range(first, min(first + 3, GC)):
+                    rows = [take_piece(lambda t, tr=tr: ug[:, :, tile_of(t, tr)].reshape(WIDE, LANES), r) for tr in (2 * h, 2 * h + 1, RING)]
+                    got.append(jnp.concatenate(rows, axis=0))
+                rhs = jnp.concatenate(merge_three(*got), axis=1)
                 for mc in range(2):
                     rows = pl.ds(BOND * mc, BOND)
                     res = jnp.dot(lh[h, rows, :], rhs, preferred_element_type=F32).astype(BF16)
-                    for rr in range(2):
-                        xs[2 * pos + rr, rows, :] = res[:, LANES * rr:LANES * rr + LANES]
+                    for rr, val in enumerate(split_three(res[:, :LANES], res[:, LANES:])[:len(got)]):
+                        xs[h * GC + first + rr, rows, :] = val
 
         def named(name, call):
             def run():
@@ -372,15 +412,18 @@
             gather({"P": early, "Q": named("late", late), "L": named("left", left_half)})
 
         def some_rows(ap, carry):
-            for pr in range(4):
+            for pr in range(RING):
+                spots = [ap * GC + 2 * pr + aa for aa in range(2)]
+                both = []
                 for h in range(2):
-                    starts = [pl.multiple_of((ap * 8 + 2 * pr + aa) * 32 + PAIR * h, PAIR) for aa in range(2)]
-                    rhs = jnp.concatenate([xs[:, pl.ds(start, PAIR), :].reshape(256, LANES) for start in starts], axis=1)
-                    res = jnp.dot(wbig[h], rhs, preferred_element_type=F32).astype(BF16)
-                    for aa in range(2):
-                        rows = pl.ds(pl.multiple_of((ap * 8 + 2 * pr + aa) * PAIR, PAIR), PAIR)
-                        for k in range(PAIR):
-                            ys[rows, pl.ds((PAIR * h + k) * LANES, LANES)] = res[PAIR * k:PAIR * k + PAIR, LANES * aa:LANES * aa + LANES]
+                    rhs = jnp.concatenate([xs[:, pl.ds(pl.multiple_of(spot * 32 + PAIR * h, PAIR), PAIR), :].reshape(WIDE, LANES) for spot in spots], axis=1)
+                    both.append(jnp.dot(wbig[h], rhs, preferred_element_type=F32).astype(BF16))
+                for aa, spot in enumerate(spots):
+                    rows = pl.ds(pl.multiple_of(spot * PAIR, PAIR), PAIR)
+                    terms = [res[PAIR * k:PAIR * k + PAIR, LANES * aa:LANES * aa + LANES] for res in both for k in range(PAIR)]
+                    for m in range(11):
+                        for side, val in enumerate(merge_three(*terms[3 * m:3 * m + 3])):
+                            ys[rows, pl.ds(WIDE * m + LANES * side, LANES)] = val
             return carry
 
         xo, xu, xd = wrap4(x + 2), wrap4(x + 1), wrap4(x - 1)
@@ -388,14 +431,14 @@
         def sigma(cols):
             for half in range(2):
                 res = lax.dot_general(rt[pl.ds(320 * half, 320), :], ys[cols, :], (((1,), (1,)), ((), ())), preferred_element_type=F32)
-                for idx in range(4):
+                for idx in range(RING):
                     part[2 * half + idx // 2, idx % 2, :, cols] = res[idx * COLS:idx * COLS + COLS]
 
         class Chunk:
             def __init__(self, num, start, width):
                 cols = self.cols = pl.ds(start, width)
                 self.rows = start // LANES, (start + width) // LANES
-                self.swap = remote(part.at[:, 1 - core, :, cols], rd.at[:, :, cols], d_s.at[num], d_r.at[num], partner)
+                self.swap = remote(part.at[:, 1 - label, :, cols], rd.at[:, :, cols], d_s.at[num], d_r.at[num], partner)
                 plan = ((xo, lo, ra, lo, x_up), (xo, hi, rb, lo, x_dn), (xu, hi, fl, hi, x_up), (xd, lo, fr, lo, x_dn), (xu, lo, fl, lo, x_up), (xd, hi, fr, hi, x_dn))
                 self.copies = [remote(ssum.at[chip, rows, cols], dst.at[to, cols], ring_s.at[6 * num + idx], ring_r.at[6 * num + idx], dev)
                                for idx, (chip, rows, dst, to, dev) in enumerate(plan)]
@@ -409,15 +452,15 @@
 
             def add(self):
                 self.swap.wait()
-                for chip in range(4):
-                    ssum[chip, :, self.cols] = part[chip, core, :, self.cols] + rd[chip, :, self.cols]
-                for cp in self.copies[:4]:
+                for chip in range(RING):
+                    ssum[chip, :, self.cols] = part[chip, label, :, self.cols] + rd[chip, :, self.cols]
+                for cp in self.copies[:RING]:
                     cp.start()
 
             def pass_on(self):
                 self.copies[0].wait_recv()
                 ssum[xu, lo, self.cols] = ssum[xu, lo, self.cols] + ra[:, self.cols]
-                self.copies[4].start()
+                self.copies[RING].start()
                 self.copies[1].wait_recv()
                 ssum[xd, hi, self.cols] = ssum[xd, hi, self.cols] + rb[:, self.cols]
                 self.copies[5].start()
@@ -429,7 +472,7 @@
                 for cp in self.copies:
                     cp.wait_send()
 
-        one, two, three = (Chunk(*spec) for spec in ((0, 0, 256), (1, 256, 256), (2, 512, LANES)))
+        one, two, three = (Chunk(*spec) for spec in ((0, 0, WIDE), (1, WIDE, WIDE), (2, 512, LANES)))
         with jax.named_scope("w0"):
             one.make_y()
         with jax.named_scope("r0"):
@@ -484,7 +527,7 @@
             inv = 1.0 / beta_new
             vt[nxt] = (sig[...] - alpha * vt[cur]) * inv
             fin[pl.ds(COLS, 1), :] = jnp.broadcast_to(alpha, (1, BOND))
-            fin[pl.ds(COLS + 8, 1), :] = jnp.broadcast_to(inv, (1, BOND))
+            fin[pl.ds(COLS + GC, 1), :] = jnp.broadcast_to(inv, (1, BOND))
             alphas[step] = alpha[0, 0]
             betas[step] = beta_new[0, 0]
         return beta_new
@@ -500,12 +543,12 @@
     vm = pltpu.VMEM
     block = (COLS, BOND)
     scratch = [
-        vm((4, 2, 160, BOND), BF16), vm((2, 1280, 768), BF16), vm((2, 256, 256), BF16), vm((TERMS, LANES, BOND), BF16), vm((BOND, 4096), BF16),
-        vm((4, 4, 25, PAIR, LANES), BF16), vm((PAIR, 1280, LANES), BF16), vm((BOND, 4096), BF16), vm((4, 2) + block, F32),
-        vm((4,) + block, F32), vm((4,) + block, F32), vm((ROWS, BOND), F32), vm((ROWS, BOND), F32), vm(block, F32), vm(block, F32),
-        vm((LANES, BOND), F32), vm((BOND, LANES), F32), vm((3, BOND, LANES), F32), vm((8, COLS, LANES), F32), vm((8, COLS, LANES), F32), vm(block, F32),
+        vm((RING, 2, 160, BOND), BF16), vm((2, 1280, 768), BF16), vm((2, WIDE, WIDE), BF16), vm((2816, BOND), BF16), vm((BOND, 2816), BF16),
+        vm((RING, RING, 25, PAIR, LANES), BF16), vm((PAIR, 1280, LANES), BF16), vm((BOND, 2816), BF16), vm((RING, 2) + block, F32),
+        vm((RING,) + block, F32), vm((RING,) + block, F32), vm((ROWS, BOND), F32), vm((ROWS, BOND), F32), vm(block, F32), vm(block, F32),
+        vm((LANES, BOND), F32), vm((BOND, LANES), F32), vm((3, BOND, LANES), F32), vm((GC, COLS, LANES), F32), vm((GC, COLS, LANES), F32), vm(block, F32),
         vm((LANES, 2, LANES), F32),
-    ] + [dma((num,)) for num in (8, 8, 8, 8, 8, 8, 4 * GSEM, 4 * GSEM, 3, 3, 18, 18)] + [dma, dma, dma((3,))]
+    ] + [dma((num,)) for num in (GC, GC, GC, GC, GC, GC, RING * GSEM, RING * GSEM, 3, 3, 18, 18)] + [dma, dma, dma((3,)), pltpu.SemaphoreType.REGULAR]
     scal = jax.ShapeDtypeStruct((NUM_STEPS,), F32)
     return pl.pallas_call(
         kernel,
@@ -523,7 +566,7 @@
         psi = wave_rows.reshape(COLS, BOND)
         left = jnp.transpose(left_rows, (1, 0, 2)).reshape(160, BOND)
         vecs, alphas, betas = run_kernel(psi, left, op_pair.reshape(512, PAIR), left_order(), right_env)
-        return vecs.reshape(7, 5, 4, 4, BOND), alphas, betas
+        return vecs.reshape(7, 5, RING, RING, BOND), alphas, betas
 
     rows = "rows"
     return jax.shard_map(local_run, mesh=mesh, in_specs=(P(rows), P(None, rows), P(), P()), out_specs=(P(None, rows), P(), P()), check_vma=False)

time: 286 us -> 273 us (0.955)
  Pallas kernels: 278 us -> 265 us
    pallas_call x1, Pallas kernels: 278 us -> 265 us  [run_kernel(): pl.pallas_call(kernel, out_shape=(jax.ShapeDtypeStruct((NUM_STEPS + 1,) +...]
where the time goes in v6:
time: 273 us
  Pallas kernels  265 us (97%)
  local copies, waits for them, and re-layouts  7 us (3%)
    pallas_call x1, Pallas kernels, run_kernel(): pl.pallas_call(kernel, out_shape=(jax.ShapeDtypeStruct((NUM_STEPS + 1,) +...  265 us

profile of v6, /device:TPU:1, one launch (start us, length us, event | category | flops | bytes accessed | tf_op | source)
XLA Modules:
  0.0 272.8 jit_solution(2958232300095224344)
XLA Ops:
  0.6 1.6 copy.8
  2.3 1.7 reshape.18.psi
  3.9 265.2 %lanczos.1 = (f32[7,80,640]{2,1,0:T(8,128)}, f32[6]{0:T(128)}, f32[6]{0:T(128)}) custom-call(f32[80,640]{1,0:T(8,128)} %reshape.18.psi, bf16[160,640]{1,0:T(8,128)(2,1)} %bitcast.5, bf16[512,16]{1,0:T(8,128)(2,1)} %bitcast.4, bf16[640,1024]{1,0:T(8,128)(2,1)} %constant.2.clone.order, bf16[32,640,640]{2,1,0:T(8,128)(2,1)} %right.1), custom_call_target="tpu_custom_call" | custom-call | tf_op jit(solution)/shard_map/lanczos/pallas_call | solution.py:553
  269.1 0.0 copy-start.1
  269.1 0.0 copy-start
  269.1 2.7 reshape.21
  271.8 0.0 copy-done.1
  271.8 0.5 copy.11
  272.3 0.0 copy-done
  272.3 0.5 copy.12
Async XLA Ops:
  269.1 2.7 copy-start.1
  269.1 3.2 %copy-start = (f32[6]{0:T(128)S(1)}, f32[6]{0:T(128)}, u32[]{:S(2)}) copy-start(f32[6]{0:T(128)} %get-tuple-element.14) | copy-start | bytes 76

commit v7 on v6

--- a/solution.py
+++ b/solution.py
@@ -19,7 +19,7 @@
 GC, RING, WIDE = 8, 4, 256
 VEC = BOND * BOND * PAIR
 PARTS = ((((0, 4), (4, 3)), ((7, 4), (11, 4))), (((15, 2), (17, 3)), ((20, 3), (23, 2))))
-ORDER = "001000P1111001Q10011010L1L01"
+ORDER = "001000P1111001Q1001101R0L1L01"
 GSEM = 30
 FARTHEST = sorted(itertools.product(range(4), range(4), range(4), range(2)), key=lambda off: -sum(min(d, 4 - d) for d in off))[:-1]
 
@@ -82,7 +82,7 @@
     return out
 
 
-def kernel(psi, left, pair, order, right, vecs, alphas, betas, lall, lh, wbig, rtmp, rt, ug, xs, ys, part, rd, ssum, ra, rb, fl, fr, fin,
+def kernel(psi, left, pair, order_hbm, right, vecs, alphas, betas, order, lall, lh, wbig, rtmp, rt, ug, xs, ys, part, rd, ssum, ra, rb, fl, fr, fin,
            sig, vt, piece_buf, out_recv, outv, stat, psi_s, psi_r, l_s, l_r, out_s, out_r, g_s, g_r, d_s, d_r,
            ring_s, ring_r, a_s, a_r, loc, ready):
     me = lax.axis_index("rows")
@@ -123,7 +123,7 @@
     partner = me + 1 - 2 * core
     places = ([wrap4(z + d) * 32 for d in range(RING)], [wrap4(y + d) * GC for d in range(RING)], [wrap4(x + d) * 2 for d in range(RING)], (core, 1 - core))
     x_up, x_dn = i * GC + wrap4(x + 1) * 2 + 1 - core, i * GC + wrap4(x - 1) * 2 + 1 - core
-    left_up, left_dn, left_far = (i * GC + wrap4(x + d) * 2 + core for d in (1, -1, 2))
+    left_up, left_dn = (i * GC + wrap4(x + d) * 2 + core for d in (1, -1))
     my_rows = rows_of(t_me)
 
     def fetch_right(first, last, row, width):
@@ -139,6 +139,8 @@
     lax.fori_loop(0, 10, fetch_right(2, LANES + COLS, 48, 32), 0)
     cp_l = pltpu.make_async_copy(left, lall.at[x, core], loc.at[1])
     cp_l.start()
+    cp_order = pltpu.make_async_copy(order_hbm, order, loc.at[3])
+    cp_order.start()
 
     row_lane = lax.broadcasted_iota(jnp.int32, (1, LANES), 1)
 
@@ -174,7 +176,7 @@
         ref = lall.at[src[0], src[1], rows]
         return remote(ref, ref, l_s.at[idx], l_r.at[idx], dev)
 
-    every = pl.ds(0, 160)
+    every, low, high = pl.ds(0, 160), pl.ds(0, COLS), pl.ds(COLS, COLS)
 
     def psi_pieces():
         for jj in range(GC):
@@ -195,7 +197,6 @@
         cp_l.wait()
         l_copy((x, core), every, 0, left_up).start()
         l_copy((x, core), every, 1, left_dn).start()
-        l_copy((x, core), every, 2, left_far).start()
         l_copy((x, core), every, RING, partner).start()
 
     def turn_right():
@@ -217,9 +218,15 @@
     lower, upper, far = (wrap4(x - 1), core), (wrap4(x + 1), core), (wrap4(x + 2), core)
 
     def left_forward():
-        for idx, (block, way) in enumerate(((lower, left_up), (upper, left_dn), (far, left_far))):
+        for idx, (block, way, rows) in enumerate(((lower, left_up, low), (upper, left_dn, high))):
             l_copy(block, every, idx, way).wait_recv()
-            l_copy(block, every, 5 + idx, partner).start()
+            l_copy(block, rows, idx + 2, way).start()
+            l_copy(block, every, idx + 5, partner).start()
+
+    def left_far():
+        l_copy(far, low, 2, partner).wait_recv()
+        l_copy(far, high, 3, partner).wait_recv()
+        l_copy(far, every, 7, partner).start()
 
     def start_up():
         with jax.named_scope("psi"):
@@ -247,8 +254,11 @@
     def left_finish():
         for idx, dx in ((RING, 0), (5, 3), (6, 1), (7, 2)):
             l_copy((wrap4(x + dx), 1 - core), every, idx, partner).wait_recv()
-        for idx in (0, 1, 2, RING, 5, 6, 7):
-            l_copy((x, core), every, idx, partner).wait_send()
+        for idx, rows in enumerate((every, every, low, high) + (every,) * RING):
+            l_copy((x, core), rows, idx, partner).wait_send()
+
+        cp_order.wait()
+
         def body(t, carry):
             rows = pl.ds(pl.multiple_of(t * 160, 160), 160)
             res = jnp.dot(lall[t // 2, t % 2], order[...], preferred_element_type=F32).astype(BF16)
@@ -378,12 +388,15 @@
         def early():
             pl.when(step == 0)(left_forward)
 
-        def late():
-            pl.when(step == 0)(left_finish)
+        def middle():
+            pl.when(step == 0)(left_far)
 
             @pl.when(step > 0)
             def _():
                 out_finish(step)
+
+        def late():
+            pl.when(step == 0)(left_finish)
 
         halves = iter(range(2))
 
@@ -409,7 +422,7 @@
             return run
 
         with jax.named_scope("gather"):
-            gather({"P": early, "Q": named("late", late), "L": named("left", left_half)})
+            gather({"P": early, "Q": middle, "R": named("late", late), "L": named("left", left_half)})
 
         def some_rows(ap, carry):
             for pr in range(RING):
@@ -444,7 +457,8 @@
                                for idx, (chip, rows, dst, to, dev) in enumerate(plan)]
 
             def make_y(self):
-                lax.fori_loop(*self.rows, some_rows, 0)
+                for group in range(*self.rows):
+                    some_rows(group, 0)
 
             def make(self):
                 sigma(self.cols)
@@ -543,17 +557,18 @@
     vm = pltpu.VMEM
     block = (COLS, BOND)
     scratch = [
+        vm((BOND, 1024), BF16),
         vm((RING, 2, 160, BOND), BF16), vm((2, 1280, 768), BF16), vm((2, WIDE, WIDE), BF16), vm((2816, BOND), BF16), vm((BOND, 2816), BF16),
         vm((RING, RING, 25, PAIR, LANES), BF16), vm((PAIR, 1280, LANES), BF16), vm((BOND, 2816), BF16), vm((RING, 2) + block, F32),
         vm((RING,) + block, F32), vm((RING,) + block, F32), vm((ROWS, BOND), F32), vm((ROWS, BOND), F32), vm(block, F32), vm(block, F32),
         vm((LANES, BOND), F32), vm((BOND, LANES), F32), vm((3, BOND, LANES), F32), vm((GC, COLS, LANES), F32), vm((GC, COLS, LANES), F32), vm(block, F32),
         vm((LANES, 2, LANES), F32),
-    ] + [dma((num,)) for num in (GC, GC, GC, GC, GC, GC, RING * GSEM, RING * GSEM, 3, 3, 18, 18)] + [dma, dma, dma((3,)), pltpu.SemaphoreType.REGULAR]
+    ] + [dma((num,)) for num in (GC, GC, GC, GC, GC, GC, RING * GSEM, RING * GSEM, 3, 3, 18, 18)] + [dma, dma, dma((RING,)), pltpu.SemaphoreType.REGULAR]
     scal = jax.ShapeDtypeStruct((NUM_STEPS,), F32)
     return pl.pallas_call(
         kernel,
         out_shape=(jax.ShapeDtypeStruct((NUM_STEPS + 1,) + block, F32), scal, scal),
-        in_specs=[vmem, anys, vmem, vmem, anys],
+        in_specs=[vmem, anys, vmem, anys, anys],
         out_specs=(anys, smem, smem),
         scratch_shapes=scratch,
         compiler_params=pltpu.CompilerParams(collective_id=0, has_side_effects=True, vmem_limit_bytes=67043328),

time: 273 us -> 267 us (0.978)
  Pallas kernels: 265 us -> 259 us
    pallas_call x1, Pallas kernels: 265 us -> 259 us  [run_kernel(): pl.pallas_call(kernel, out_shape=(jax.ShapeDtypeStruct((NUM_STEPS + 1,) +...]
where the time goes in v7:
time: 267 us; the launch traced here: 266 us
  Pallas kernels  259 us (97%)
  local copies, waits for them, and re-layouts  7 us (3%)
    pallas_call x1, Pallas kernels, run_kernel(): pl.pallas_call(kernel, out_shape=(jax.ShapeDtypeStruct((NUM_STEPS + 1,) +...  259 us

profile of v7, /device:TPU:1, one launch (start us, length us, event | category | flops | bytes accessed | tf_op | source)
XLA Modules:
  0.0 266.5 jit_solution(13537595083312692204)
XLA Ops:
  0.6 1.6 copy.8
  2.3 1.7 reshape.18.psi
  3.9 258.8 %lanczos.1 = (f32[7,80,640]{2,1,0:T(8,128)}, f32[6]{0:T(128)}, f32[6]{0:T(128)}) custom-call(f32[80,640]{1,0:T(8,128)} %reshape.18.psi, bf16[160,640]{1,0:T(8,128)(2,1)} %bitcast.5, bf16[512,16]{1,0:T(8,128)(2,1)} %bitcast.4, bf16[640,1024]{1,0:T(8,128)(2,1)} %constant.2.clone.order_hbm, bf16[32,640,640]{2,1,0:T(8,128)(2,1)} %right.1), custom_call_target="tpu_custom_call" | custom-call | tf_op jit(solution)/shard_map/lanczos/pallas_call | solution.py:568
  262.8 0.0 copy-start.1
  262.8 0.0 copy-start
  262.8 2.7 reshape.21
  265.4 0.0 copy-done.1
  265.4 0.5 copy.11
  265.9 0.0 copy-done
  266.0 0.5 copy.12
Async XLA Ops:
  262.8 2.7 %copy-start.1 = (f32[6]{0:T(128)S(1)}, f32[6]{0:T(128)}, u32[]{:S(2)}) copy-start(f32[6]{0:T(128)} %get-tuple-element.13) | copy-start | bytes 76
  262.8 3.2 %copy-start = (f32[6]{0:T(128)S(1)}, f32[6]{0:T(128)}, u32[]{:S(2)}) copy-start(f32[6]{0:T(128)} %get-tuple-element.14) | copy-start | bytes 76

commit v8 on v7

--- a/solution.py
+++ b/solution.py
@@ -19,7 +19,7 @@
 GC, RING, WIDE = 8, 4, 256
 VEC = BOND * BOND * PAIR
 PARTS = ((((0, 4), (4, 3)), ((7, 4), (11, 4))), (((15, 2), (17, 3)), ((20, 3), (23, 2))))
-ORDER = "001000P1111001Q1001101R0L1L01"
+ORDER = "0011000P111001Q1001101R0L1L01"
 GSEM = 30
 FARTHEST = sorted(itertools.product(range(4), range(4), range(4), range(2)), key=lambda off: -sum(min(d, 4 - d) for d in off))[:-1]
 
@@ -311,12 +311,12 @@
         wait((1, 0), 0, 2)
         second(2, 0)
         yield
-        second_forward(0)
-        yield
         wait((2, 0), 0, RING)
         second(3, 0)
         wait((2, 0), 1, 5)
         second(3, 1)
+        yield
+        second_forward(0)
         yield
         for b in range(1, RING):
             second_forward(b)

time: 267 us -> 263 us (0.985)
  Pallas kernels: 259 us -> 255 us
    pallas_call x1, Pallas kernels: 259 us -> 255 us  [run_kernel(): pl.pallas_call(kernel, out_shape=(jax.ShapeDtypeStruct((NUM_STEPS + 1,) +...]
where the time goes in v8:
time: 263 us; the launch traced here: 262 us
  Pallas kernels  255 us (97%)
  local copies, waits for them, and re-layouts  7 us (3%)
    pallas_call x1, Pallas kernels, run_kernel(): pl.pallas_call(kernel, out_shape=(jax.ShapeDtypeStruct((NUM_STEPS + 1,) +...  255 us

profile of v8, /device:TPU:1, one launch (start us, length us, event | category | flops | bytes accessed | tf_op | source)
XLA Modules:
  0.0 262.4 jit_solution(13780343256720510531)
XLA Ops:
  0.6 1.6 copy.8
  2.3 1.7 reshape.18.psi
  3.9 254.7 %lanczos.1 = (f32[7,80,640]{2,1,0:T(8,128)}, f32[6]{0:T(128)}, f32[6]{0:T(128)}) custom-call(f32[80,640]{1,0:T(8,128)} %reshape.18.psi, bf16[160,640]{1,0:T(8,128)(2,1)} %bitcast.5, bf16[512,16]{1,0:T(8,128)(2,1)} %bitcast.4, bf16[640,1024]{1,0:T(8,128)(2,1)} %constant.2.clone.order_hbm, bf16[32,640,640]{2,1,0:T(8,128)(2,1)} %right.1), custom_call_target="tpu_custom_call" | custom-call | tf_op jit(solution)/shard_map/lanczos/pallas_call | solution.py:568
  258.7 0.0 copy-start.1
  258.7 0.0 copy-start
  258.7 2.7 %reshape.21 = f32[7,5,4,4,640]{4,3,2,1,0:T(4,128)} reshape(f32[7,80,640]{2,1,0:T(8,128)} %get-tuple-element.6) | data formatting | bytes 2867200 | tf_op jit(solution)/shard_map/reshape | solution.py:584
  261.3 0.0 copy-done.1
  261.3 0.5 copy.11
  261.9 0.0 copy-done
  261.9 0.5 copy.12
Async XLA Ops:
  258.7 2.7 %copy-start.1 = (f32[6]{0:T(128)S(1)}, f32[6]{0:T(128)}, u32[]{:S(2)}) copy-start(f32[6]{0:T(128)} %get-tuple-element.13) | copy-start | bytes 76
  258.7 3.2 %copy-start = (f32[6]{0:T(128)S(1)}, f32[6]{0:T(128)}, u32[]{:S(2)}) copy-start(f32[6]{0:T(128)} %get-tuple-element.14) | copy-start | bytes 76

commit v9 on v8

--- a/solution.py
+++ b/solution.py
@@ -486,7 +486,7 @@
                 for cp in self.copies:
                     cp.wait_send()
 
-        one, two, three = (Chunk(*spec) for spec in ((0, 0, WIDE), (1, WIDE, WIDE), (2, 512, LANES)))
+        one, two, three = (Chunk(*spec) for spec in ((0, 0, LANES), (1, LANES, WIDE), (2, 3 * LANES, WIDE)))
         with jax.named_scope("w0"):
             one.make_y()
         with jax.named_scope("r0"):

time: 263 us -> 261 us (level)
  no operation moved by 1% of the time
where the time goes in v9:
time: 261 us
  Pallas kernels  253 us (97%)
  local copies, waits for them, and re-layouts  7 us (3%)
    pallas_call x1, Pallas kernels, run_kernel(): pl.pallas_call(kernel, out_shape=(jax.ShapeDtypeStruct((NUM_STEPS + 1,) +...  253 us

profile of v9, /device:TPU:1, one launch (start us, length us, event | category | flops | bytes accessed | tf_op | source)
XLA Modules:
  0.0 260.7 jit_solution(14115012838896560424)
XLA Ops:
  0.6 1.6 copy.8
  2.3 1.7 reshape.18.psi
  3.9 253.0 %lanczos.1 = (f32[7,80,640]{2,1,0:T(8,128)}, f32[6]{0:T(128)}, f32[6]{0:T(128)}) custom-call(f32[80,640]{1,0:T(8,128)} %reshape.18.psi, bf16[160,640]{1,0:T(8,128)(2,1)} %bitcast.5, bf16[512,16]{1,0:T(8,128)(2,1)} %bitcast.4, bf16[640,1024]{1,0:T(8,128)(2,1)} %constant.2.clone.order_hbm, bf16[32,640,640]{2,1,0:T(8,128)(2,1)} %right.1), custom_call_target="tpu_custom_call" | custom-call | tf_op jit(solution)/shard_map/lanczos/pallas_call | solution.py:568
  256.9 0.0 copy-start.1
  257.0 0.0 copy-start
  257.0 2.7 %reshape.21 = f32[7,5,4,4,640]{4,3,2,1,0:T(4,128)} reshape(f32[7,80,640]{2,1,0:T(8,128)} %get-tuple-element.6) | data formatting | bytes 2867200 | tf_op jit(solution)/shard_map/reshape | solution.py:584
  259.6 0.0 copy-done.1
  259.6 0.5 copy.11
  260.1 0.0 copy-done
  260.1 0.5 copy.12
Async XLA Ops:
  256.9 2.7 %copy-start.1 = (f32[6]{0:T(128)S(1)}, f32[6]{0:T(128)}, u32[]{:S(2)}) copy-start(f32[6]{0:T(128)} %get-tuple-element.13) | copy-start | bytes 76
  257.0 3.2 %copy-start = (f32[6]{0:T(128)S(1)}, f32[6]{0:T(128)}, u32[]{:S(2)}) copy-start(f32[6]{0:T(128)} %get-tuple-element.14) | copy-start | bytes 76
